TPU v7x, 256 devices: a whole 4x4x8 slice. The times are simulated.
256 devices in a mesh: rep: 4 (over x_lo, core), shard: 64 (over z, x_hi, y).
Axes of the slice: x: 4 (x_hi: 2, x_lo: 2; x = x_hi * 2 + x_lo), y: 4, z: 8, core: 2. Of those that a mesh axis runs over, the one named last changes fastest.
Arguments:
- dense_out: bfloat16 [32768, 128], P(('rep', 'shard')), may hold values from -0.75 to 0.75
- pooled: bfloat16 [32768, 26, 128], P(('rep', 'shard')), may hold values from -0.75 to 0.75
- top_weight: bfloat16 [479, 1024], replicated, may hold values from -0.25 to 0.25
- top_cotangent: bfloat16 [32768, 1024], P(('rep', 'shard')), may hold values from -3 to 3
- indices: int32 [32768, 26, 2], P(('rep', 'shard')), may hold values from 0 to 16383, as said below
Outputs:
- dense_grad: bfloat16 [32768, 128], P(('rep', 'shard'))
- top_grad: float32 [479, 1024], replicated
- bias_grad: float32 [1024], replicated
- table_grad: float32 [26, 16384, 128], P(None, 'shard')
Inputs may be any that keep to these rules, and one draw needn't show every extreme that they name: `indices`: rows r with r // 256 = s are held by shard s. For every device's 128 samples and every table, at most 2 of the device's lookups fall in any one block of 64 rows starting at a multiple of 64, and some such block holds exactly 2.
All inputs are finite; a program needn't handle non-finite values.
Results may differ from a plain program's by a relative error of at most 0.008.
Values may be sent and summed in bfloat16 or wider, within the bound.
A program may use at most 128 MiB of HBM per device.

v0:
```python
import jax
import jax.numpy as jnp
import numpy as np
from jax import lax
from jax.sharding import PartitionSpec as P

R_SHARD = 256


def cut_along(shard, dim, devices):
    dims = shard.shape
    blocks = shard.reshape(*dims[:dim], devices, dims[dim] // devices, *dims[dim + 1 :])
    return jnp.moveaxis(blocks, dim, 0)


def summed_on_arrival(shard, axis, dim):
    devices = lax.axis_size(axis)
    blocks = lax.all_to_all(cut_along(shard, dim, devices), axis, 0, 0, tiled=True)
    return jnp.sum(blocks, axis=0)


def sent_to_all(shard, axis):
    copies = jnp.broadcast_to(shard, (lax.axis_size(axis), *shard.shape))
    return lax.all_to_all(copies, axis, split_axis=0, concat_axis=0, tiled=True)


def of_everyone(shard, axis):
    everything = sent_to_all(shard, axis)
    return jnp.sum(everything, axis=0)


def packed_total(arrays, axis):
    ravelled, at, outs = (jnp.concatenate([a.reshape(-1) for a in arrays]), 0, [])
    subtotal = of_everyone(ravelled, axis)
    for a in arrays:
        outs.append(subtotal[at : at + a.size].reshape(a.shape))
        at += a.size
    return tuple(outs)


def laid_out(blocks, dim):
    dims = list(blocks.shape[1:])
    dims[dim] *= blocks.shape[0]
    return jnp.moveaxis(blocks, 0, dim).reshape(dims)


def gather_together(arrays, axis, dims):
    ravelled = jnp.concatenate([a.reshape(-1) for a in arrays])
    lines, at, outs = (lax.all_gather(ravelled, axis), 0, [])
    for a, dim in zip(arrays, dims):
        blocks = lines[:, at : at + a.size].reshape(-1, *a.shape)
        outs.append(laid_out(blocks, dim))
        at += a.size
    return tuple(outs)


def exchange_both(shard, axis, axes, splits, concats):
    sizes = [lax.axis_size(a) for a in axes]
    blocks = cut_along(shard, splits[0], sizes[0])
    blocks = jnp.moveaxis(cut_along(blocks, splits[1] + 1, sizes[1]), 0, 1)
    inside = blocks.shape[2:]
    blocks = blocks.reshape(-1, *inside)
    blocks = lax.all_to_all(blocks, axis, split_axis=0, concat_axis=0, tiled=True)
    blocks = laid_out(blocks.reshape(*sizes, *inside), concats[0] + 1)
    return laid_out(blocks, concats[1])


def one_hot_sums(rows, keys, height):
    tables_here = rows.shape[0]
    flat_rows = rows.reshape(tables_here, -1, rows.shape[-1])
    flat_keys = keys.reshape(tables_here, -1)

    def per_table(member):
        table_rows, table_keys = member
        levels = lax.broadcasted_iota(jnp.int32, (height, table_keys.shape[0]), 0)
        matches = (levels == table_keys[None, :]).astype(jnp.bfloat16)
        return jnp.dot(matches, table_rows, preferred_element_type=jnp.float32)

    return lax.map(per_table, (flat_rows, flat_keys))


def pair_table(vectors):
    lower_i, lower_j = np.tril_indices(vectors, -1)
    select = np.zeros((vectors * vectors, lower_i.shape[0]), np.float32)
    select[lower_i * vectors + lower_j, np.arange(lower_i.shape[0])] = 1.0
    mirrored = np.zeros((lower_i.shape[0], vectors * vectors), np.float32)
    mirrored[np.arange(lower_i.shape[0]), lower_i * vectors + lower_j] = 1.0
    mirrored[np.arange(lower_i.shape[0]), lower_j * vectors + lower_i] = 1.0
    return (jnp.asarray(select), jnp.asarray(mirrored))


def on_device(dense_out, pooled, top_weight, top_cotangent, indices):
    samples = dense_out.shape[0]
    emb_width = dense_out.shape[1]
    tables = pooled.shape[1]
    lookups = indices.shape[2]
    replicas = lax.axis_size("rep")
    shards = lax.axis_size("shard")
    vectors = tables + 1
    select, mirrored = pair_table(vectors)
    stacked = jnp.concatenate([dense_out[:, None, :], pooled], axis=1)
    gram_matrix = jnp.einsum("bie,bje->bij", stacked, stacked, preferred_element_type=jnp.float32)
    gram_flat = gram_matrix.reshape(samples, vectors * vectors)
    pair_values = jnp.dot(gram_flat, select, preferred_element_type=jnp.float32).astype(
        jnp.bfloat16
    )
    joined = jnp.concatenate([dense_out, pair_values], axis=1)
    grad_in = lax.dot_general(
        top_cotangent, top_weight, (((1,), (1,)), ((), ())), preferred_element_type=jnp.float32
    )
    top_part = lax.dot_general(
        joined, top_cotangent, (((0,), (0,)), ((), ())), preferred_element_type=jnp.float32
    )
    bias_part = jnp.sum(top_cotangent, axis=0, dtype=jnp.float32)
    pair_grad = grad_in[:, emb_width:]
    mirror = jnp.dot(pair_grad, mirrored, preferred_element_type=jnp.float32).reshape(
        samples, vectors, vectors
    )
    mirror_high = mirror.astype(jnp.bfloat16)
    mirror_low = (mirror - mirror_high.astype(jnp.float32)).astype(jnp.bfloat16)
    vec_grad = jnp.einsum("bij,bje->bie", mirror_high, stacked, preferred_element_type=jnp.float32)
    vec_grad = vec_grad + jnp.einsum(
        "bij,bje->bie", mirror_low, stacked, preferred_element_type=jnp.float32
    )
    dense_grad = (grad_in[:, :emb_width] + vec_grad[:, 0]).astype(jnp.bfloat16)
    pooled_grad = vec_grad[:, 1:].astype(jnp.bfloat16)
    row_span = R_SHARD // replicas
    blocks = replicas * shards
    per_block = 2 * samples * lookups // blocks
    count_here = samples * lookups
    capacity = blocks * per_block
    by_table = jnp.transpose(indices, (1, 0, 2)).reshape(tables, count_here)
    lookup_rows = jnp.broadcast_to(
        jnp.transpose(pooled_grad, (1, 0, 2))[:, :, None, :], (tables, samples, lookups, emb_width)
    ).reshape(tables, count_here, emb_width)

    def place_table(member):
        table_keys, table_rows = member
        block_row = table_keys // row_span
        later = lax.broadcasted_iota(jnp.int32, (count_here, count_here), 0)
        sooner = lax.broadcasted_iota(jnp.int32, (count_here, count_here), 1)
        earlier = (block_row[None, :] == block_row[:, None]) & (sooner < later)
        slot_row = block_row * per_block + jnp.sum(earlier, axis=1, dtype=jnp.int32)
        levels = lax.broadcasted_iota(jnp.int32, (capacity, count_here), 0)
        placed = levels == slot_row[None, :]
        rows_out = jnp.dot(
            placed.astype(jnp.bfloat16), table_rows, preferred_element_type=jnp.float32
        ).astype(jnp.bfloat16)
        keys_out = (
            jnp.sum(
                jnp.where(placed, (table_keys % R_SHARD + 1)[None, :], 0), axis=1, dtype=jnp.int32
            )
            - 1
        )
        return (rows_out, keys_out)

    send_rows, send_keys = lax.map(place_table, (by_table, lookup_rows))
    top_share, bias_share = (
        summed_on_arrival(top_part, "shard", 1),
        summed_on_arrival(bias_part, "shard", 0),
    )
    top_share, bias_share = packed_total((top_share, bias_share), "rep")
    top_grad, bias_grad = gather_together((top_share, bias_share), "shard", (1, 0))
    blocked_rows = send_rows.reshape(tables, shards, replicas, per_block, emb_width)
    blocked_keys = send_keys.reshape(tables, shards, replicas, per_block)
    got_rows, got_keys = (
        exchange_both(blocked_rows, ("rep", "shard"), ("rep", "shard"), (2, 1), (2, 1)),
        exchange_both(blocked_keys, ("rep", "shard"), ("rep", "shard"), (2, 1), (2, 1)),
    )
    local_keys = got_keys - lax.axis_index("rep") * row_span
    partial_value = one_hot_sums(got_rows, local_keys, row_span)
    table_grad = lax.all_gather(partial_value, "rep", axis=1, tiled=True)
    return (dense_grad, top_grad, bias_grad, table_grad)


def solution(mesh):
    return jax.shard_map(
        on_device,
        mesh=mesh,
        in_specs=(
            P(("rep", "shard"), None),
            P(("rep", "shard"), None, None),
            P(),
            P(("rep", "shard"), None),
            P(("rep", "shard"), None, None),
        ),
        out_specs=(P(("rep", "shard"), None), P(), P(), P(None, "shard", None)),
        check_vma=False,
    )
```

profile of v0, /device:TPU:1, one launch (start us, length us, event | category | flops | bytes accessed | tf_op | source)
XLA Modules:
  0.0 357.7 jit_solution(951075348307605910)
XLA Ops:
  9.0 15.1 %all-to-all-start.1 = ((f32[64,1,16]{2,1,0:T(1,128)}), f32[64,1,16]{2,1,0:T(1,128)S(1)}, u32[]{:S(2)}, u32[]{:S(2)}) async-start(f32[64,1,16]{2,1,0:T(1,128)} %bitcast.15), calls=%async_computation.1 | async-start | bytes 65536 | tf_op jit(solution)/shard_map/all_to_all | solution.py:18
  31.1 1.8 fusion.16
  32.9 2.8 copy.177
  37.3 1.8 fusion.15
  39.1 3.0 copy.178
  42.1 2.7 reshape.151
  48.7 1.8 fusion.19
  51.4 12.3 %all-to-all-start = ((f32[64,479,16]{1,2,0:T(8,128)}), f32[64,479,16]{1,2,0:T(8,128)S(1)}, u32[]{:S(2)}, u32[]{:S(2)}) async-start(f32[64,479,16]{1,2,0:T(8,128)} %bitcast.14), calls=%async_computation | async-start | bytes 4194304 | tf_op jit(solution)/shard_map/all_to_all | solution.py:18
  63.7 2.3 broadcast_in_dim.71
  66.1 58.4 %while.25 = (s32[]{:T(128)}, bf16[26,512,128]{2,1,0:T(8,128)(2,1)}, s32[26,512]{1,0:T(8,128)S(1)}, s32[26,256]{1,0:T(8,128)S(1)}, bf16[26,256,128]{2,1,0:T(8,128)(2,1)}, /*index=5*/s32[]{:T(128)}, s32[]{:T(128)}) while((s32[]{:T(128)}, bf16[26,512,128]{2,1,0:T(8,128)(2,1)}, s32[26,512]{1,0:T(8,128)S(1)}, s32[26,256]{1,0:T(8,128)S(1)}, ...), condition=%wide.region_7.8_spmd, body=%wide.region_4.7_spmd.sunk | while | flops 34486784 | bytes 224349 | solution.py:157
  125.5 13.6 %all-to-all-start.3 = ((s32[256,26,1,1,2]{1,4,3,2,0:T(2,128)}), s32[256,26,1,1,2]{1,4,3,2,0:T(2,128)S(1)}, u32[]{:S(2)}, u32[]{:S(2)}) async-start(s32[256,26,1,1,2]{1,4,3,2,0:T(2,128)} %bitcast.27), calls=%async_computation.3 | async-start | bytes 524288 | tf_op jit(solution)/shard_map/all_to_all | solution.py:63
  139.6 14.9 %all-to-all-done.3 = s32[256,26,1,1,2]{1,4,3,2,0:T(2,128)S(1)} async-done(((s32[256,26,1,1,2]{1,4,3,2,0:T(2,128)}), s32[256,26,1,1,2]{1,4,3,2,0:T(2,128)S(1)}, u32[]{:S(2)}, u32[]{:S(2)}) %all-to-all-start.3) | async-done | bytes 53280 | tf_op jit(solution)/shard_map/all_to_all | solution.py:63
  155.2 4.1 %all-to-all-start.2 = ((f32[4,1,7680]{2,1,0:T(1,128)}), f32[4,1,7680]{2,1,0:T(1,128)S(1)}, u32[]{:S(2)}, u32[]{:S(2)}) async-start(f32[4,1,7680]{2,1,0:T(1,128)} %broadcast_in_dim.67), calls=%async_computation.2 | async-start | bytes 245760 | tf_op jit(solution)/shard_map/all_to_all | solution.py:24
  159.3 3.0 copy.195
  162.3 5.3 %copy.196 = bf16[256,26,1,1,2,128]{5,4,1,3,2,0:T(2,128)(2,1)} copy(bf16[256,26,1,1,2,128]{5,0,4,1,3,2:T(8,128)(2,1)S(1)} %bitcast.110) | data formatting | bytes 6815744 | tf_op jit(solution)/shard_map/reshape | solution.py:62
  167.5 6.7 %all-to-all-start.4 = ((bf16[256,26,1,1,2,128]{5,4,1,3,2,0:T(2,128)(2,1)}), bf16[256,26,1,1,2,128]{5,4,1,3,2,0:T(2,128)(2,1)}, u32[]{:S(2)}, u32[]{:S(2)}) async-start(bf16[256,26,1,1,2,128]{5,4,1,3,2,0:T(2,128)(2,1)} %copy.196), calls=%async_computation.4 | async-start | bytes 6815744 | tf_op jit(solution)/shard_map/all_to_all | solution.py:63
  176.0 81.5 %all-to-all-done.4 = bf16[256,26,1,1,2,128]{5,4,1,3,2,0:T(2,128)(2,1)} async-done(((bf16[256,26,1,1,2,128]{5,4,1,3,2,0:T(2,128)(2,1)}), bf16[256,26,1,1,2,128]{5,4,1,3,2,0:T(2,128)(2,1)}, u32[]{:S(2)}, u32[]{:S(2)}) %all-to-all-start.4) | async-done | bytes 3407904 | tf_op jit(solution)/shard_map/all_to_all | solution.py:63
  257.5 2.8 copy.197
  260.3 5.3 %copy.198 = bf16[26,64,1,4,2,128]{5,4,3,1,0,2:T(2,128)(2,1)} copy(bf16[26,64,1,4,2,128]{5,1,3,4,0,2:T(8,128)(2,1)S(1)} %bitcast.111) | data formatting | bytes 6815744 | tf_op jit(solution)/shard_map/transpose | solution.py:44
  265.6 43.5 %while.26 = (s32[]{:T(128)}, f32[26,64,128]{2,1,0:T(8,128)}, s32[26,512]{1,0:T(8,128)S(1)}, bf16[26,512,128]{2,1,0:T(8,128)(2,1)}, s32[]{:T(128)}) while((s32[]{:T(128)}, f32[26,64,128]{2,1,0:T(8,128)}, s32[26,512]{1,0:T(8,128)S(1)}, bf16[26,512,128]{2,1,0:T(8,128)(2,1)}, s32[]{:T(128)}) %tuple.84), condition=%wide.region_9.10_spmd, body=%wide.region_8.9_spmd.sunk | while | flops 8421378 | bytes 171081 | solution.py:79
  312.4 2.6 copy.185
  315.0 3.9 %copy.186 = f32[479,64,16]{0,2,1:T(8,128)S(1)} copy(f32[479,64,16]{1,2,0:T(8,128)} %bitcast.109) | data formatting | bytes 3923968 | tf_op jit(solution)/shard_map/transpose | solution.py:44
  321.4 25.4 %all-gather.5.cloned.1.call-done = f32[26,256,128]{2,1,0:T(8,128)} async-done(((f32[26,64,128]{2,1,0:T(8,128)}), f32[26,256,128]{2,1,0:T(8,128)}) %all-gather.5.cloned.1.call-update) | async-done | bytes 3407888 | tf_op jit(solution)/shard_map/all_gather | solution.py:172
  346.7 4.1 %copy.231 = f32[26,256,128]{2,1,0:T(8,128)} copy(f32[26,256,128]{2,1,0:T(8,128)} %all-gather.5.cloned.1.call-done) | data formatting | bytes 6815744
  (354 shorter events, 125.1 us)
Async XLA Ops:
  7.2 17.0 %copy-start = (bf16[479,1024]{1,0:T(8,128)(2,1)S(1)}, bf16[479,1024]{1,0:T(8,128)(2,1)}, u32[]{:S(2)}) copy-start(bf16[479,1024]{1,0:T(8,128)(2,1)} %param.13) | copy-start | bytes 2942980
  7.2 18.3 %copy-start.6 = (bf16[351,729]{1,0:T(8,128)(2,1)S(1)}, bf16[351,729]{1,0:T(8,128)(2,1)}, u32[]{:S(2)}) copy-start(bf16[351,729]{1,0:T(8,128)(2,1)} %constant.168) | copy-start | bytes 1535278
  9.0 42.4 %all-to-all-start.1 = ((f32[64,1,16]{2,1,0:T(1,128)}), f32[64,1,16]{2,1,0:T(1,128)S(1)}, u32[]{:S(2)}, u32[]{:S(2)}) async-start(f32[64,1,16]{2,1,0:T(1,128)} %bitcast.15), calls=%async_computation.1 | async-start | bytes 65536 | tf_op jit(solution)/shard_map/all_to_all | solution.py:18
  25.9 3.4 copy-start.7
  39.1 5.7 %copy-start.2 = (f32[128,27,128]{0,2,1:T(8,128)S(1)}, f32[128,27,128]{0,2,1:T(8,128)}, u32[]{:S(2)}) copy-start(f32[128,27,128]{0,2,1:T(8,128)} %copy.177) | copy-start | bytes 5308420
  44.8 3.1 copy-start.5
  46.5 1.2 copy-start.3
  47.7 0.9 copy-start.4
  47.9 2.6 copy-start.8
  51.4 74.1 %all-to-all-start = ((f32[64,479,16]{1,2,0:T(8,128)}), f32[64,479,16]{1,2,0:T(8,128)S(1)}, u32[]{:S(2)}, u32[]{:S(2)}) async-start(f32[64,479,16]{1,2,0:T(8,128)} %bitcast.14), calls=%async_computation | async-start | bytes 4194304 | tf_op jit(solution)/shard_map/all_to_all | solution.py:18
  125.5 29.0 %all-to-all-start.3 = ((s32[256,26,1,1,2]{1,4,3,2,0:T(2,128)}), s32[256,26,1,1,2]{1,4,3,2,0:T(2,128)S(1)}, u32[]{:S(2)}, u32[]{:S(2)}) async-start(s32[256,26,1,1,2]{1,4,3,2,0:T(2,128)} %bitcast.27), calls=%async_computation.3 | async-start | bytes 524288 | tf_op jit(solution)/shard_map/all_to_all | solution.py:63
  155.2 12.4 %all-to-all-start.2 = ((f32[4,1,7680]{2,1,0:T(1,128)}), f32[4,1,7680]{2,1,0:T(1,128)S(1)}, u32[]{:S(2)}, u32[]{:S(2)}) async-start(f32[4,1,7680]{2,1,0:T(1,128)} %broadcast_in_dim.67), calls=%async_computation.2 | async-start | bytes 245760 | tf_op jit(solution)/shard_map/all_to_all | solution.py:24
  167.5 90.0 %all-to-all-start.4 = ((bf16[256,26,1,1,2,128]{5,4,1,3,2,0:T(2,128)(2,1)}), bf16[256,26,1,1,2,128]{5,4,1,3,2,0:T(2,128)(2,1)}, u32[]{:S(2)}, u32[]{:S(2)}) async-start(bf16[256,26,1,1,2,128]{5,4,1,3,2,0:T(2,128)(2,1)} %copy.196), calls=%async_computation.4 | async-start | bytes 6815744 | tf_op jit(solution)/shard_map/all_to_all | solution.py:63
  174.3 136.4 %all-gather.7.cloned.1.call-start = ((), (), s32[]{:S(2)}) async-start(), calls=%async_computation.6 | async-start | bytes 1996800 | tf_op jit(solution)/shard_map/all_gather | solution.py:49
  175.8 171.0 %all-gather.5.cloned.1.call-start = ((), (), s32[]{:S(2)}) async-start(), calls=%async_computation.5 | async-start | bytes 4259840 | tf_op jit(solution)/shard_map/all_gather | solution.py:172
  320.7 30.1 %copy-start.1 = (bf16[479,1024]{1,0:T(8,128)(2,1)S(1)}, bf16[479,1024]{1,0:T(8,128)(2,1)}, u32[]{:S(2)}) copy-start(bf16[479,1024]{1,0:T(8,128)(2,1)} %param.13) | copy-start | bytes 2942980
Sparse Core Ops, SparseCore 0:
  178.7 120.9 all-gather.6
  309.2 37.4 all-gather.4
where the time goes:
time: 360 us; the launch traced here: 358 us
  waiting for transfers between devices  122 us (34%)
  matrix products  97.8 us (27%)
  local copies, waits for them, and re-layouts  55.8 us (16%)
  starting transfers between devices  52.3 us (15%)
  between operations  14.4 us (4%)
  other arithmetic  14.2 us (4%)
    all_to_all x2, waiting for transfers between devices, exchange_both(): lax.all_to_all(blocks, axis, split_axis=0, concat_axis=0, tiled=True)  96.3 us
    dot_general x26, matrix products, place_table(): jnp.dot(placed.astype(jnp.bfloat16), table_rows, preferred_element_type=j...  45.3 us
    dot_general x26, matrix products, per_table(): return jnp.dot(matches, table_rows, preferred_element_type=jnp.float32)  43.3 us
    all_to_all x2, starting transfers between devices, summed_on_arrival(): lax.all_to_all(cut_along(shard, dim, devices), axis, 0, 0, tiled=True)  27.4 us
    all_gather x1, waiting for transfers between devices, on_device(): table_grad = lax.all_gather(partial_value, 'rep', axis=1, tiled=True)  25.4 us
    all_to_all x2, starting transfers between devices, exchange_both(): lax.all_to_all(blocks, axis, split_axis=0, concat_axis=0, tiled=True)  20.4 us
    unnamed x25, local copies, waits for them, and re-layouts  12.4 us
    transpose x2, local copies, waits for them, and re-layouts, laid_out(): return jnp.moveaxis(blocks, 0, dim).reshape(dims)  9.16 us
  transfers between devices with their start and end apart: 7, of which 3 were waited for; matrix products, arithmetic and copies ran while one was open for 45% of the time, Pallas kernels for 0%

commit v1 on v0

v1 whole, which is shorter than its diff:
```python
import functools

import jax
import jax.numpy as jnp
from jax import lax
from jax.experimental import pallas as pl
from jax.experimental.pallas import tpu as pltpu
from jax.sharding import PartitionSpec as P

F32=jnp.float32; BF=jnp.bfloat16
NT=(((1,),(1,)),((),()))
def coords():
    r=lax.axis_index("rep"); s=lax.axis_index("shard")
    return (s//4)%2*2+r//2, s%4, s//8, r%2
def local_kernel(dense, pooled, w, cot, idx, dgrad, top, rows, vt, g, gt, cd, kacc):
    x,y,z,c=coords()
    i0=lax.broadcasted_iota(jnp.int32,(128,128),0); i1=lax.broadcasted_iota(jnp.int32,(128,128),1)
    eye=(i0==i1).astype(F32).astype(BF)
    vt[0]=lax.dot_general(eye,dense[...],NT,preferred_element_type=F32)
    def tr(i,_):
        vt[i+1]=lax.dot_general(eye,pooled[i],NT,preferred_element_type=F32)
        return 0
    lax.fori_loop(0,26,tr,0,unroll=2)
    gt[0:479]=lax.dot_general(w[...],cot[...],NT,preferred_element_type=F32)
    gt[479:480]=jnp.zeros((1,128),F32)
    g[0:128]=vt[0]
    g[479:480]=jnp.ones((1,128),F32)
    def prow(a,b):
        hi=jnp.maximum(a,b); lo=jnp.minimum(a,b)
        return 128+hi*(hi-1)//2+lo
    def gram(i,_):
        va=vt[i]
        for d in range(1,14):
            j=i+d
            j=jnp.where(j>=27,j-27,j)
            s=jnp.sum(va*vt[j],axis=0,keepdims=True)
            g[pl.ds(prow(i,j),1),:]=s
        return 0
    lax.fori_loop(0,27,gram,0)
    top[...]=jnp.dot(g[...].astype(BF),cot[...],preferred_element_type=F32).astype(top.dtype)
    blk=idx[...]//64
    sh=idx[...]//256
    j4=blk-sh*4
    z_=sh//8; xh=(sh//4)%2; y_=sh%4
    x_=xh*2+j4//2; c_=j4%2
    slot=(((x_^x)*4+(y_^y))*2+(c_^c))*16+((z_-z+8)%8)*2
    key=idx[...]%64+1
    cd[0:26]=blk.astype(F32)
    cd[26:52]=slot.astype(F32)
    cd[52:78]=key.astype(F32)
    kacc[...]=jnp.zeros_like(kacc)
    lt=i0<i1
    s512=lax.broadcasted_iota(jnp.int32,(512,128),0).astype(F32)
    def dense_out(_):
        pass
    def vg(i):
        acc=jnp.zeros((128,128),F32)
        for j in range(27):
            p=jnp.where(i==j,479,prow(i,jnp.int32(j)))
            acc=acc+gt[pl.ds(p,1),:]*vt[j]
        return acc
    d0=vg(jnp.int32(0))+gt[0:128]
    dgrad[...]=lax.dot_general(eye,d0.astype(BF),NT,preferred_element_type=F32).astype(BF)
    def table(t,_):
        v=vg(t+1).astype(BF)
        b=cd[t]
        bt=jnp.concatenate([b,jnp.zeros((126,128),F32)],axis=0).T
        c0=bt[:,0:1]; c1=bt[:,1:2]
        one=jnp.float32(1); zero=jnp.float32(0)
        r0=jnp.sum(jnp.where((c0==b[0:1])&lt,one,zero),axis=0,keepdims=True)
        r1=jnp.sum(jnp.where(c0==b[1:2],one,zero)+jnp.where((c1==b[1:2])&lt,one,zero),axis=0,keepdims=True)
        sl=cd[t+26]
        P0=jnp.where(s512==sl[0:1]+r0,one,zero).astype(BF)
        P1=jnp.where(s512==sl[1:2]+r1,one,zero).astype(BF)
        P=jnp.concatenate([P0,P1],axis=1)
        kv=cd[t+52]
        R=jnp.where(i0==t,kv[0:1],zero).astype(BF); R1=jnp.where(i0==t,kv[1:2],zero).astype(BF)
        rhs=jnp.concatenate([jnp.concatenate([v,v],axis=1),jnp.concatenate([R,R1],axis=1)],axis=0)
        o=lax.dot_general(P,rhs,NT,preferred_element_type=F32)
        rows[t+1]=o[:,0:128].astype(BF)
        kacc[...]+=o[:,128:256]
        return 0
    lax.fori_loop(0,26,table,0)
    rows[0]=kacc[...].astype(BF)

def local_call(dense, pooled_t, w, cot, idx_t):
    vm=pl.BlockSpec(memory_space=pltpu.VMEM)
    return pl.pallas_call(local_kernel,
        out_shape=(jax.ShapeDtypeStruct((128,128),BF),jax.ShapeDtypeStruct((480,1024),F32),jax.ShapeDtypeStruct((27,512,128),BF)),
        in_specs=[vm]*5,out_specs=(vm,)*3,
        scratch_shapes=[pltpu.VMEM((27,128,128),F32),pltpu.VMEM((480,128),F32),pltpu.VMEM((480,128),F32),pltpu.VMEM((78,2,128),F32),pltpu.VMEM((512,128),F32)],
        compiler_params=pltpu.CompilerParams(vmem_limit_bytes=40*2**20),name="local")(dense,pooled_t,w,cot,idx_t)

MESH=pl.DeviceIdType.MESH
T=3; NC=9; E=T*NC
def xor4(a,b):
    al=a%2; ah=a//2; bl=b%2; bh=b//2
    return ((ah+bh)%2)*2+(al+bl)%2
def dev(x,y,z,c):
    return ((x%2)*2+c, z*8+(x//2)*4+y)
def plane_peer(q):
    x,y,z,c=coords()
    return dev(xor4(x,q//8),xor4(y,(q//2)%4),z,(c+q)%2)
def z_peer(d):
    x,y,z,c=coords()
    return dev(x,y,(z+d+8)%8,c)
def rep_peer(i):
    x,y,z,c=coords()
    r=(x%2)*2+c
    return (xor4(r,i), z*8+(x//2)*4+y)
def comm_kernel(rows, out, rv, kt, D, zr, fin, s_send, s_recv, z_send, z_recv, a_send, a_recv):
    bar=pltpu.get_barrier_semaphore()
    def sig(q,_):
        pl.semaphore_signal(bar,1,device_id=plane_peer(q),device_id_type=MESH)
        return 0
    lax.fori_loop(1,32,sig,0)
    for d in (1,-1):
        pl.semaphore_signal(bar,1,device_id=z_peer(d),device_id_type=MESH)
    pl.semaphore_wait(bar,33)
    def s_chunk(ch,_):
        def s_one(q,_):
            pltpu.make_async_remote_copy(src_ref=rows.at[pl.ds(ch*T,T),pl.ds(q*16,16)],dst_ref=rv.at[pl.ds(ch*T,T),pl.ds(q*16,16)],
               send_sem=s_send.at[ch],recv_sem=s_recv.at[ch],device_id=plane_peer(q),device_id_type=MESH).start()
            return 0
        lax.fori_loop(1,32,s_one,0)
        return 0
    lax.fori_loop(0,NC,s_chunk,0)
    def zcopy(dirn, step, ch):
        rel=(5-step) if dirn==0 else (3+step)
        if step==1:
            lo=32*dirn; sz=32
        else:
            lo=0; sz=64
        return pltpu.make_async_remote_copy(
            src_ref=D.at[pl.ds(ch*T,T),rel,pl.ds(lo,sz)],dst_ref=zr.at[dirn,step-1,pl.ds(ch*T,T),pl.ds(lo,sz)],
            send_sem=z_send.at[dirn,step-1,ch],recv_sem=z_recv.at[dirn,step-1,ch],
            device_id=z_peer(1 if dirn==0 else -1),device_id_type=MESH)
    def acopy(i,ch):
        r=lax.axis_index("rep")
        return pltpu.make_async_remote_copy(
            src_ref=fin.at[pl.ds(ch*T,T)],dst_ref=out.at[pl.ds(ch*T,T),pl.ds(pl.multiple_of(r*64,64),64)],
            send_sem=a_send.at[i-1,ch],recv_sem=a_recv.at[i-1,ch],device_id=rep_peer(i),device_id_type=MESH)
    rowi=lax.broadcasted_iota(jnp.int32,(512,512),0).astype(F32)
    def step(k,_):
        @pl.when(k<NC)
        def _():
            ch=k
            reg=rv.at[pl.ds(ch*T,T),pl.ds(16,496)]
            pltpu.make_async_copy(reg,reg,s_recv.at[ch]).wait()
            rv[pl.ds(ch*T,T),0:16]=rows[pl.ds(ch*T,T),0:16]
            @pl.when(ch==0)
            def _():
                i0=lax.broadcasted_iota(jnp.int32,(128,128),0); i1=lax.broadcasted_iota(jnp.int32,(128,128),1)
                eye=(i0==i1).astype(F32).astype(BF)
                kk=lax.dot_general(eye,rv[0],NT,preferred_element_type=F32)
                zz=(lax.broadcasted_iota(jnp.int32,(128,512),1)%16//2*64).astype(F32)
                kt[...]=jnp.where(kk>0.5,kk-1+zz,-1.0)
            def acc(t,_):
                e=ch*T+t
                kr=kt[pl.ds((e+127)%128,1),:]
                oh=jnp.where(rowi==kr,jnp.float32(1),jnp.float32(0)).astype(BF)
                d=jnp.dot(oh,rv[e],preferred_element_type=F32).astype(BF)
                D[e]=d.reshape(8,64,128)
                return 0
            lax.fori_loop(0,T,acc,0)
            zcopy(0,1,ch).start(); zcopy(1,1,ch).start()
        for s in (1,2,3):
            @pl.when((k>=s)&(k<NC+s))
            def _(s=s):
                ch=k-s
                for dirn in (0,1):
                    zcopy(dirn,s,ch).wait_recv()
                    rel=(4-s) if dirn==0 else (4+s)
                    lo,sz=(32*dirn,32) if s==1 else (0,64)
                    for t in range(T):
                        e=ch*T+t
                        D[e,rel,lo:lo+sz]=(D[e,rel,lo:lo+sz].astype(F32)+zr[dirn,s-1,e,lo:lo+sz].astype(F32)).astype(BF)
                    zcopy(dirn,s+1,ch).start()
        @pl.when((k>=4)&(k<NC+4))
        def _():
            ch=k-4
            r=lax.axis_index("rep")
            zcopy(0,4,ch).wait_recv(); zcopy(1,4,ch).wait_recv()
            for t in range(T):
                e=ch*T+t
                v=(D[e,0].astype(F32)+zr[0,3,e].astype(F32)+zr[1,3,e].astype(F32)).astype(BF)
                fin[e]=v
                out[e,pl.ds(pl.multiple_of(r*64,64),64)]=v
            for i in (1,2,3): acopy(i,ch).start()
        return 0
    lax.fori_loop(0,NC+4,step,0)
    def drain(ch,_):
        for i in (1,2,3):
            acopy(i,ch).wait()
        for dirn in (0,1):
            for s in (1,2,3,4): zcopy(dirn,s,ch).wait_send()
        reg=rows.at[pl.ds(ch*T,T),pl.ds(16,496)]
        pltpu.make_async_copy(reg,reg,s_send.at[ch]).wait()
        return 0
    lax.fori_loop(0,NC,drain,0)

def comm_call(rows):
    vm=pl.BlockSpec(memory_space=pltpu.VMEM)
    return pl.pallas_call(comm_kernel,out_shape=jax.ShapeDtypeStruct((E,256,128),BF),in_specs=[vm],out_specs=vm,
      scratch_shapes=[pltpu.VMEM((E,512,128),BF),pltpu.VMEM((128,512),F32),pltpu.VMEM((E,8,64,128),BF),pltpu.VMEM((2,4,E,64,128),BF),pltpu.VMEM((E,64,128),BF),
        pltpu.SemaphoreType.DMA((NC,)),pltpu.SemaphoreType.DMA((NC,)),
        pltpu.SemaphoreType.DMA((2,4,NC)),pltpu.SemaphoreType.DMA((2,4,NC)),pltpu.SemaphoreType.DMA((3,NC)),pltpu.SemaphoreType.DMA((3,NC))],
      compiler_params=pltpu.CompilerParams(collective_id=1,has_side_effects=True,vmem_limit_bytes=56*2**20),name="comm")(rows)

def on_device(dense_out, pooled, top_weight, top_cotangent, indices):
    dgrad, top, rows = local_call(dense_out, jnp.transpose(pooled,(1,0,2)), top_weight, top_cotangent, jnp.transpose(indices,(1,2,0)))
    table = comm_call(rows)
    top = lax.psum(top, ("rep", "shard"))
    return dgrad, top[:479], top[479], table[1:].astype(F32)


def solution(mesh):
    both = P(("rep", "shard"))
    return jax.shard_map(on_device, mesh=mesh, in_specs=(both, both, P(), both, both),
        out_specs=(both, P(), P(), P(None, "shard", None)), check_vma=False)
```

time: 360 us -> 325 us (0.903)
  Pallas kernels: 0 us -> 102 us
  matrix products: 97.8 us -> 0 us
  waiting for transfers between devices: 122 us -> 192 us
  starting transfers between devices: 52.3 us -> 0.04 us
  local copies, waits for them, and re-layouts: 55.8 us -> 11 us
  other arithmetic: 14.2 us -> 3.6 us
    psum x0 -> x1, waiting for transfers between devices: none -> 192 us  [on_device(): top = lax.psum(top, ('rep', 'shard'))]
    pallas_call x0 -> x2, Pallas kernels: none -> 102 us  [the longest x1 79.1 us: comm_call(): pl.pallas_call(comm_kernel, out_shape=jax.ShapeDtypeStruct((E, 256, 128),...]
    dot_general x59 -> x0, matrix products: 97.8 us -> none  [the longest x26 45.3 us: place_table(): jnp.dot(placed.astype(jnp.bfloat16), table_rows, preferred_element_type=j...]
    all_to_all x5 -> x0, waiting for transfers between devices: 96.3 us -> none  [the longest x2 96.3 us: exchange_both(): lax.all_to_all(blocks, axis, split_axis=0, concat_axis=0, tiled=True)]
    all_to_all x5 -> x0, starting transfers between devices: 51.9 us -> none  [the longest x2 27.4 us: summed_on_arrival(): lax.all_to_all(cut_along(shard, dim, devices), axis, 0, 0, tiled=True)]
    all_gather x2 -> x0, waiting for transfers between devices: 25.4 us -> none  [the longest x1 25.4 us: on_device(): table_grad = lax.all_gather(partial_value, 'rep', axis=1, tiled=True)]
    transpose x5 -> x0, local copies, waits for them, and re-layouts: 10.1 us -> none  [the longest x2 9.16 us: laid_out(): return jnp.moveaxis(blocks, 0, dim).reshape(dims)]
    reduce_sum x56 -> x0, other arithmetic: 10 us -> none  [the longest x26 4.72 us: place_table(): slot_row = block_row * per_block + jnp.sum(earlier, axis=1, dtype=jnp.int32)]
  transfers between devices with their start and end apart: 7 -> 1, of which waited for: 3 -> 1; matrix products, arithmetic and copies ran while one was open for 45% -> 1% of each run, Pallas kernels for 0% -> 24%
where the time goes in v1:
time: 325 us; the launch traced here: 323 us
  waiting for transfers between devices  192 us (59%)
  Pallas kernels  102 us (31%)
  between operations  14.1 us (4%)
  local copies, waits for them, and re-layouts  11 us (3%)
  other arithmetic  3.6 us (1%)
    psum x1, waiting for transfers between devices, on_device(): top = lax.psum(top, ('rep', 'shard'))  192 us
    pallas_call x1, Pallas kernels, comm_call(): pl.pallas_call(comm_kernel, out_shape=jax.ShapeDtypeStruct((E, 256, 128),...  79.1 us
    pallas_call x1, Pallas kernels, local_call(): pl.pallas_call(local_kernel, out_shape=(jax.ShapeDtypeStruct((128, 128),...  22.8 us
    unnamed x13, local copies, waits for them, and re-layouts  9.6 us
  transfers between devices with their start and end apart: 1, of which 1 were waited for; matrix products, arithmetic and copies ran while one was open for 1% of the time, Pallas kernels for 24%

profile of v1, /device:TPU:1, one launch (start us, length us, event | category | flops | bytes accessed | tf_op | source)
XLA Modules:
  0.0 323.1 jit_solution(2767102123487555334)
XLA Ops:
  7.2 0.0 all-reduce.2.cloned.1.call-start
  7.2 0.0 copy-start.1
  7.2 1.2 copy-done.1
  8.4 0.0 copy-start.2
  8.4 1.2 copy-done.2
  9.6 0.0 copy-start.3
  9.6 0.9 copy-done.3
  10.5 0.0 copy-start.4
  10.5 0.8 copy-done.4
  11.3 0.0 copy-start.5
  11.3 0.7 copy-done.5
  12.0 22.8 %local.1 = (bf16[128,128]{1,0:T(8,128)(2,1)}, f32[480,1024]{1,0:T(8,128)}, bf16[27,512,128]{2,1,0:T(8,128)(2,1)S(1)}) custom-call(bf16[128,128]{1,0:T(8,128)(2,1)S(1)} %copy-done.4, bf16[26,128,128]{2,1,0:T(8,128)(2,1)S(1)} %bitcast.4, bf16[479,1024]{1,0:T(8,128)(2,1)S(1)} %copy-done.1, bf16[128,1024]{1,0:T(8,128)(2,1)S(1)} %copy-done.3, ...), custom_call_target="tpu_custom_call" | custom-call | tf_op jit(solution)/shard_map/local/pallas_call | solution.py:88
  34.9 0.0 copy-start
  34.9 1.8 copy-done
  36.6 0.0 all-reduce.2.cloned.1.call-update
  36.6 79.1 %comm.1 = bf16[27,256,128]{2,1,0:T(8,128)(2,1)} custom-call(bf16[27,512,128]{2,1,0:T(8,128)(2,1)} %copy-done), custom_call_target="tpu_custom_call" | custom-call | tf_op jit(solution)/shard_map/comm/pallas_call | solution.py:204
  115.8 3.6 %slice_convert_fusion = f32[26,256,128]{2,1,0:T(8,128)} fusion(bf16[27,256,128]{2,1,0:T(8,128)(2,1)} %comm.1), kind=kLoop, calls=%fused_computation | loop fusion | flops 851968 | bytes 5111808 | tf_op jit(solution)/shard_map/convert_element_type | solution.py:214
  119.4 192.5 %all-reduce.2.cloned.1.call-done = f32[480,1024]{1,0:T(8,128)} async-done(((f32[480,1024]{1,0:T(8,128)}), f32[480,1024]{1,0:T(8,128)}) %all-reduce.2.cloned.1.call-update) | async-done | bytes 1966096 | tf_op jit(solution)/shard_map/psum | solution.py:213
  311.9 1.4 slice.13
  313.2 3.0 copy.10
Async XLA Ops:
  7.2 304.7 %all-reduce.2.cloned.1.call-start = ((), (), s32[]{:S(2)}) async-start(), calls=%async_computation | async-start | bytes 3932160 | tf_op jit(solution)/shard_map/psum | solution.py:213
  7.2 1.2 copy-start.1
  8.4 1.2 copy-start.2
  9.6 0.9 copy-start.3
  10.5 0.8 copy-start.4
  11.3 0.7 copy-start.5
  34.9 1.8 copy-start
Sparse Core Ops, SparseCore 0:
  36.8 275.0 all-reduce.1

commit v2 on v0

v2 whole, which is shorter than its diff:
```python
import jax
import jax.numpy as jnp
from jax import lax
from jax.experimental import pallas as pl
from jax.experimental.pallas import tpu as pltpu
F32 = jnp.float32
BF = jnp.bfloat16
NT = (((1,), (1,)), ((), ()))
MESH = pl.DeviceIdType.MESH
SIZES = (2, 3, 3, 3, 3, 3, 3, 3, 3)
NC = len(SIZES)
STARTS = tuple(sum(SIZES[:i]) for i in range(NC))
NT_ = 26
AHEAD = 3
HOOK = (1, 3, 5, 6, 9)
RELAY = True


def coords():
    r = lax.axis_index("rep")
    s = lax.axis_index("shard")
    return (s // 4) % 2 * 2 + r // 2, s % 4, s // 8, r % 2


def xor4(a, b):
    return ((a // 2 + b // 2) % 2) * 2 + (a % 2 + b % 2) % 2


def dev(x, y, z, c):
    return ((x % 2) * 2 + c, z * 8 + (x // 2) * 4 + y)


def plane_peer(q):
    x, y, z, c = coords()
    return dev(xor4(x, q // 8), xor4(y, (q // 2) % 4), z, (c + q) % 2)


def z_peer(d):
    x, y, z, c = coords()
    return dev(x, y, (z + d + 8) % 8, c)


def rep_peer(i):
    x, y, z, c = coords()
    return (xor4((x % 2) * 2 + c, i), z * 8 + (x // 2) * 4 + y)


def rcopy(src, dst, ss, rs, to):
    return pltpu.make_async_remote_copy(
        src_ref=src, dst_ref=dst, send_sem=ss, recv_sem=rs, device_id=to, device_id_type=MESH)


def kernel(dense_h, pool_h, w_h, cot_h, idx_h, dgrad, topo, bias, tab,
           dense, pool, w, cot, idx, vt, g, gt, sl, cs, keyt, krow, krv, kt,
           rows, rv, D, zr, fin, tb, tp, r0, h, r1, s1, r2, f64,
           in_sem, s_send, s_recv, z_send, z_recv, a_send, a_recv, t_send, t_recv):
    x, y, z, c = coords()
    rep = (x % 2) * 2 + c
    ins = [pltpu.make_async_copy(a, b, in_sem.at[i]) for i, (a, b) in enumerate(
        ((idx_h, idx), (pool_h, pool), (dense_h, dense), (cot_h, cot), (w_h, w)))]
    for cp in ins:
        cp.start()
    bar = pltpu.get_barrier_semaphore()

    def sig(q, _):
        pl.semaphore_signal(bar, 1, device_id=plane_peer(q), device_id_type=MESH)
        return 0

    lax.fori_loop(1, 32, sig, 0)

    def sigz(d, _):
        pl.semaphore_signal(bar, 1, device_id=z_peer(d), device_id_type=MESH)
        return 0

    lax.fori_loop(1, 8, sigz, 0)
    i0 = lax.broadcasted_iota(jnp.int32, (128, 128), 0)
    i1 = lax.broadcasted_iota(jnp.int32, (128, 128), 1)
    eye = (i0 == i1).astype(F32).astype(BF)
    one = jnp.float32(1)
    zero = jnp.float32(0)

    ins[0].wait()
    cs[...] = jnp.zeros_like(cs)
    keyt[...] = jnp.zeros_like(keyt)
    keys, slots, blks = [], [], []
    for l in range(2):
        row = idx[:, l, :]
        blk = row // 64
        sh = row // 256
        part = blk - sh * 4
        xx = (sh // 4) % 2 * 2 + part // 2
        slot = ((xor4(xx, x) * 4 + xor4(sh % 4, y)) * 2 + (part + c) % 2) * 16 + ((sh // 8 - z + 8) % 8) * 2
        keys.append((row - blk * 64 + 1).astype(F32))
        slots.append(slot.astype(F32))
        cs[32 * l:32 * l + 26] = blk.astype(F32)
    ct = cs[...].T
    ltf = jnp.where(i0 < i1, one, zero)
    for t in range(NT_):
        c0 = ct[:, t:t + 1]
        c1 = ct[:, 32 + t:33 + t]
        b0 = cs[t:t + 1]
        b1 = cs[32 + t:33 + t]
        sl[0, t:t + 1] = jnp.sum(jnp.where(c0 == b0, ltf, zero), axis=0, keepdims=True)
        sl[1, t:t + 1] = jnp.sum(jnp.where(c0 == b1, one, zero) + jnp.where(c1 == b1, ltf, zero), axis=0, keepdims=True)
    for l in range(2):
        s = sl[l] + slots[l]
        sl[l] = s
        cs[32 * l:32 * l + 26] = s
        cs[64 + 32 * l:90 + 32 * l] = keys[l]
    ct = cs[...].T
    l512 = lax.broadcasted_iota(jnp.int32, (128, 512), 1).astype(F32)
    for t in range(NT_):
        m = jnp.where(ct[:, t:t + 1] == l512, ct[:, 64 + t:65 + t], zero)
        m = m + jnp.where(ct[:, 32 + t:33 + t] == l512, ct[:, 96 + t:97 + t], zero)
        keyt[t:t + 1] = jnp.sum(m, axis=0, keepdims=True)
    krow[...] = keyt[...].T.astype(BF)

    ins[1].wait()
    ins[2].wait()
    vt[0] = lax.dot_general(eye, dense[...], NT, preferred_element_type=F32)

    def tr(i, _):
        vt[i + 1] = lax.dot_general(eye, pool[i], NT, preferred_element_type=F32)
        return 0

    lax.fori_loop(0, NT_, tr, 0, unroll=2)
    ins[3].wait()
    ins[4].wait()
    gt[0:479] = lax.dot_general(w[...], cot[...], NT, preferred_element_type=F32)
    gt[479:480] = jnp.zeros((1, 128), F32)

    pl.semaphore_wait(bar, 38)

    def k_one(q, _):
        rcopy(krow.at[pl.ds(q * 16, 16)], krv.at[pl.ds(q * 16, 16)], s_send.at[NC], s_recv.at[NC], plane_peer(q)).start()
        return 0

    lax.fori_loop(1, 32, k_one, 0)

    def prow(a, b):
        hi = jnp.maximum(a, b)
        lo = jnp.minimum(a, b)
        return 128 + hi * (hi - 1) // 2 + lo

    def vg(i):
        acc = jnp.zeros((128, 128), F32)
        for j in range(27):
            p = jnp.where(i == j, 479, prow(i, jnp.int32(j)))
            acc = acc + gt[pl.ds(p, 1), :] * vt[j]
        return acc

    s512 = lax.broadcasted_iota(jnp.int32, (512, 128), 0).astype(F32)

    def compute(ch):
        t0, n = STARTS[ch], SIZES[ch]

        def table(t, _):
            v = vg(t + 1).astype(BF)
            s0 = sl[0, pl.ds(t, 1), :]
            s1_ = sl[1, pl.ds(t, 1), :]
            p = jnp.where((s512 == s0) , one, zero) + jnp.where(s512 == s1_, one, zero)
            rows[t] = lax.dot_general(p.astype(BF), v, NT, preferred_element_type=F32).astype(BF)
            return 0

        lax.fori_loop(t0, t0 + n, table, 0)

        def s_one(q, _):
            rcopy(rows.at[pl.ds(t0, n), pl.ds(q * 16, 16)], rv.at[pl.ds(t0, n), pl.ds(q * 16, 16)],
                  s_send.at[ch], s_recv.at[ch], plane_peer(q)).start()
            return 0

        lax.fori_loop(1, 32, s_one, 0)

    def top_part():
        g[0:128] = vt[0]
        g[479:480] = jnp.ones((1, 128), F32)

        def gram(i, _):
            va = vt[i]
            for d in range(1, 14):
                j = i + d
                j = jnp.where(j >= 27, j - 27, j)
                g[pl.ds(prow(i, j), 1), :] = jnp.sum(va * vt[j], axis=0, keepdims=True)
            return 0

        lax.fori_loop(0, 27, gram, 0)
        gb = g[...].astype(BF)
        for i in range(2):
            tp[i, 0:480] = jnp.dot(gb, cot[:, 512 * i:512 * i + 512], preferred_element_type=F32).astype(BF)
            tp[i, 480:512] = jnp.zeros((32, 512), BF)

    def core_copy():
        return rcopy(tp.at[1 - c], r0, t_send.at[0], t_recv.at[0], rep_peer(1))

    def z_share(d):
        zz = (z + d) % 8
        return rcopy(h.at[pl.ds(pl.multiple_of(zz * 64, 64), 64)], r1.at[d - 1], t_send.at[1], t_recv.at[1], z_peer(d))

    def spot(ref, xx, yy):
        return ref.at[pl.ds(pl.multiple_of(xx * 16, 16), 16), pl.ds(pl.multiple_of(yy * 128, 128), 128)]

    def p_share(q):
        return rcopy(spot(s1, xor4(x, q // 4), xor4(y, q % 4)), r2.at[q - 1], t_send.at[2], t_recv.at[2], plane_peer(q * 2))

    def p_gather(q):
        return rcopy(spot(f64, x, y), spot(f64, x, y), t_send.at[3], t_recv.at[3], plane_peer(q * 2))

    def z_gather(d):
        reg = tb.at[c, pl.ds(pl.multiple_of(z * 64, 64), 64)]
        return rcopy(f64, reg, t_send.at[4], t_recv.at[4], z_peer(d))

    def core_gather():
        return rcopy(tb.at[c], tb.at[c], t_send.at[5], t_recv.at[5], rep_peer(1))

    def each(n, copy):
        def one_(i, _):
            copy(i).start()
            return 0
        lax.fori_loop(1, n, one_, 0)

    def wait_for(reg, sem):
        pltpu.make_async_copy(reg, reg, sem).wait()

    def hook0():
        core_copy().wait_recv()
        h[...] = (tp[c].astype(F32) + r0[...].astype(F32)).astype(BF)
        each(8, z_share)

    def hook1():
        wait_for(r1, t_recv.at[1])
        a = h[pl.ds(pl.multiple_of(z * 64, 64), 64)].astype(F32)
        for i in range(7):
            a = a + r1[i].astype(F32)
        s1[...] = a.astype(BF)
        each(16, p_share)

    def hook2():
        wait_for(r2, t_recv.at[2])
        a = spot(s1, x, y)[...].astype(F32)
        for i in range(15):
            a = a + r2[i].astype(F32)
        spot(f64, x, y)[...] = a.astype(BF)
        each(16, p_gather)

    def hook3():
        wait_for(r2, t_recv.at[3])
        tb[c, pl.ds(pl.multiple_of(z * 64, 64), 64)] = f64[...]
        each(8, z_gather)

    def hook4():
        wait_for(r1, t_recv.at[4])
        core_gather().start()

    hooks = dict(zip(HOOK, (hook0, hook1, hook2, hook3, hook4)))

    def zcopy(dirn, step, ch):
        t0, n = STARTS[ch], SIZES[ch]
        rel = (5 - step) if dirn == 0 else (3 + step)
        lo, sz = (32 * dirn, 32) if step == 1 else (0, 64)
        return rcopy(D.at[pl.ds(t0, n), rel, pl.ds(lo, sz)], zr.at[dirn, step - 1, pl.ds(t0, n), pl.ds(lo, sz)],
                     z_send.at[dirn, step - 1, ch], z_recv.at[dirn, step - 1, ch], z_peer(1 if dirn == 0 else -1))

    def acopy(i, ch):
        t0, n = STARTS[ch], SIZES[ch]
        reg = fin.at[pl.ds(t0, n), pl.ds(pl.multiple_of(rep * 64, 64), 64)]
        return rcopy(reg, reg, a_send.at[i - 1, ch], a_recv.at[i - 1, ch], rep_peer(i))

    def fwd(ch):
        t0, n = STARTS[ch], SIZES[ch]
        reg = fin.at[pl.ds(t0, n), pl.ds(pl.multiple_of((rep + 2) % 4 * 64, 64), 64)]
        return rcopy(reg, reg, a_send.at[2, ch], a_recv.at[2, ch], rep_peer(1))

    rowi = lax.broadcasted_iota(jnp.int32, (512, 512), 0).astype(F32)

    def gather_rows(ch):
        t0, n = STARTS[ch], SIZES[ch]
        if ch == 0:
            wait_for(krv.at[pl.ds(16, 496)], s_recv.at[NC])
            krv[0:16] = krow[0:16]
            kk = lax.dot_general(eye, krv[...], NT, preferred_element_type=F32)
            zz = (lax.broadcasted_iota(jnp.int32, (128, 512), 1) % 16 // 2 * 64).astype(F32)
            kt[...] = jnp.where(kk > 0.5, kk - 1 + zz, -1.0)
        wait_for(rv.at[pl.ds(t0, n), pl.ds(16, 496)], s_recv.at[ch])
        rv[t0:t0 + n, 0:16] = rows[t0:t0 + n, 0:16]

        def acc(t, _):
            oh = jnp.where(rowi == kt[pl.ds(t, 1), :], one, zero).astype(BF)
            D[t] = jnp.dot(oh, rv[t], preferred_element_type=F32).astype(BF).reshape(8, 64, 128)
            return 0

        lax.fori_loop(t0, t0 + n, acc, 0)
        zcopy(0, 1, ch).start()
        zcopy(1, 1, ch).start()

    def zstep(s, ch):
        t0, n = STARTS[ch], SIZES[ch]
        for dirn in (0, 1):
            zcopy(dirn, s, ch).wait_recv()
            rel = (4 - s) if dirn == 0 else (4 + s)
            lo, sz = (32 * dirn, 32) if s == 1 else (0, 64)
            for e in range(t0, t0 + n):
                D[e, rel, lo:lo + sz] = (D[e, rel, lo:lo + sz].astype(F32) + zr[dirn, s - 1, e, lo:lo + sz].astype(F32)).astype(BF)
            zcopy(dirn, s + 1, ch).start()

    def finish(ch):
        t0, n = STARTS[ch], SIZES[ch]
        zcopy(0, 4, ch).wait_recv()
        zcopy(1, 4, ch).wait_recv()
        for e in range(t0, t0 + n):
            v = D[e, 0].astype(F32) + zr[0, 3, e].astype(F32) + zr[1, 3, e].astype(F32)
            fin[e, pl.ds(pl.multiple_of(rep * 64, 64), 64)] = v.astype(BF)
        acopy(1, ch).start()
        acopy(2, ch).start()
        if not RELAY:
            acopy(3, ch).start()

    compute(0)
    top_part()
    core_copy().start()
    for ch in range(1, AHEAD):
        compute(ch)
    for k in range(NC + 4):
        if k + AHEAD < NC:
            compute(k + AHEAD)
        if k == NC - AHEAD:
            d0 = vg(jnp.int32(0)) + gt[0:128]
            dgrad[...] = lax.dot_general(eye, d0.astype(BF), NT, preferred_element_type=F32).astype(BF)
        if 0 <= k - 4 < NC:
            finish(k - 4)
        for s in (3, 2, 1):
            if 0 <= k - s < NC:
                zstep(s, k - s)
        if k < NC:
            gather_rows(k)
        if k in hooks:
            hooks[k]()
    if RELAY:
        for ch in range(NC):
            acopy(2, ch).wait_recv()
            fwd(ch).start()
    core_gather().wait_recv()
    for i in range(2):
        topo[:, 512 * i:512 * i + 512] = tb[i, 0:479].astype(F32)
        bias[:, 512 * i:512 * i + 512] = tb[i, 479:480].astype(F32)
    for ch in range(NC):
        t0, n = STARTS[ch], SIZES[ch]
        acopy(1, ch).wait_recv()
        if RELAY:
            fwd(ch).wait_recv()
        else:
            acopy(2, ch).wait_recv()
            acopy(3, ch).wait_recv()
        tab[t0:t0 + n] = fin[t0:t0 + n].astype(F32)
    for ch in range(NC):
        t0, n = STARTS[ch], SIZES[ch]
        acopy(1, ch).wait_send()
        acopy(2, ch).wait_send()
        if RELAY:
            fwd(ch).wait_send()
        else:
            acopy(3, ch).wait_send()
        for dirn in (0, 1):
            for s in (1, 2, 3, 4):
                zcopy(dirn, s, ch).wait_send()
        wait_for(rows.at[pl.ds(t0, n), pl.ds(16, 496)], s_send.at[ch])
    wait_for(krow.at[pl.ds(16, 496)], s_send.at[NC])
    core_copy().wait_send()
    wait_for(r1, t_send.at[1])
    wait_for(r2, t_send.at[2])
    wait_for(r2, t_send.at[3])
    wait_for(r1, t_send.at[4])
    core_gather().wait_send()


def fused_call(dense, pool, w, cot, idx, cid=1, name="fused"):
    vm = pl.BlockSpec(memory_space=pltpu.VMEM)
    hbm = pl.BlockSpec(memory_space=pltpu.HBM)
    dma = pltpu.SemaphoreType.DMA
    V = pltpu.VMEM
    return pl.pallas_call(
        kernel,
        out_shape=(
            jax.ShapeDtypeStruct((128, 128), BF),
            jax.ShapeDtypeStruct((479, 1024), F32),
            jax.ShapeDtypeStruct((1, 1024), F32),
            jax.ShapeDtypeStruct((26, 256, 128), F32),
        ),
        in_specs=[hbm] * 5,
        out_specs=(vm,) * 4,
        scratch_shapes=[
            V((128, 128), BF), V((26, 128, 128), BF), V((479, 1024), BF), V((128, 1024), BF), V((26, 2, 128), jnp.int32),
            V((27, 128, 128), F32), V((480, 128), F32), V((480, 128), F32), V((2, 26, 128), F32), V((128, 128), F32),
            V((128, 512), F32), V((512, 128), BF), V((512, 128), BF), V((128, 512), F32),
            V((26, 512, 128), BF), V((26, 512, 128), BF), V((26, 8, 64, 128), BF), V((2, 4, 26, 64, 128), BF), V((26, 256, 128), BF),
            V((2, 512, 512), BF), V((2, 512, 512), BF), V((512, 512), BF), V((512, 512), BF), V((7, 64, 512), BF),
            V((64, 512), BF), V((15, 16, 128), BF), V((64, 512), BF),
            dma((5,)), dma((NC + 1,)), dma((NC + 1,)), dma((2, 4, NC)), dma((2, 4, NC)), dma((3, NC)), dma((3, NC)), dma((6,)), dma((6,)),
        ],
        compiler_params=pltpu.CompilerParams(collective_id=cid, has_side_effects=True, vmem_limit_bytes=40 * 2**20),
        name=name,
    )(dense, pool, w, cot, idx)


def on_device(dense_out, pooled, top_weight, top_cotangent, indices):
    dgrad, top, bias, table = fused_call(
        dense_out, jnp.transpose(pooled, (1, 0, 2)), top_weight, top_cotangent, jnp.transpose(indices, (1, 2, 0)))
    return dgrad, top, bias.reshape(1024), table


def solution(mesh):
    from jax.sharding import PartitionSpec as P
    both = P(("rep", "shard"))
    return jax.shard_map(
        on_device, mesh=mesh, in_specs=(both, both, P(), both, both),
        out_specs=(both, P(), P(), P(None, "shard", None)), check_vma=False)
```

time: 360 us -> 123 us (0.34)
  waiting for transfers between devices: 122 us -> 0 us
  Pallas kernels: 0 us -> 113 us
  matrix products: 97.8 us -> 0 us
  starting transfers between devices: 52.3 us -> 0 us
  local copies, waits for them, and re-layouts: 55.8 us -> 9.03 us
  other arithmetic: 14.2 us -> 0 us
  between operations: 14.4 us -> 0.65 us
    pallas_call x0 -> x1, Pallas kernels: none -> 113 us  [fused_call(): pl.pallas_call(kernel, out_shape=(jax.ShapeDtypeStruct((128, 128), BF), j...]
    dot_general x59 -> x0, matrix products: 97.8 us -> none  [the longest x26 45.3 us: place_table(): jnp.dot(placed.astype(jnp.bfloat16), table_rows, preferred_element_type=j...]
    all_to_all x5 -> x0, waiting for transfers between devices: 96.3 us -> none  [the longest x2 96.3 us: exchange_both(): lax.all_to_all(blocks, axis, split_axis=0, concat_axis=0, tiled=True)]
    all_to_all x5 -> x0, starting transfers between devices: 51.9 us -> none  [the longest x2 27.4 us: summed_on_arrival(): lax.all_to_all(cut_along(shard, dim, devices), axis, 0, 0, tiled=True)]
    all_gather x2 -> x0, waiting for transfers between devices: 25.4 us -> none  [the longest x1 25.4 us: on_device(): table_grad = lax.all_gather(partial_value, 'rep', axis=1, tiled=True)]
    transpose x5 -> x0, local copies, waits for them, and re-layouts: 10.1 us -> none  [the longest x2 9.16 us: laid_out(): return jnp.moveaxis(blocks, 0, dim).reshape(dims)]
    reduce_sum x56 -> x0, other arithmetic: 10 us -> none  [the longest x26 4.72 us: place_table(): slot_row = block_row * per_block + jnp.sum(earlier, axis=1, dtype=jnp.int32)]
    reshape x6 -> x0, local copies, waits for them, and re-layouts: 9.56 us -> none  [the longest x2 6.05 us: exchange_both(): blocks = blocks.reshape(-1, *inside)]
  transfers between devices with their start and end apart: 7 -> 0, of which waited for: 3 -> 0; matrix products, arithmetic and copies ran while one was open for 45% -> 0% of each run, Pallas kernels for 0% -> 0%
where the time goes in v2:
time: 123 us; the launch traced here: 122 us
  Pallas kernels  113 us (92%)
  local copies, waits for them, and re-layouts  9.03 us (7%)
    pallas_call x1, Pallas kernels, fused_call(): pl.pallas_call(kernel, out_shape=(jax.ShapeDtypeStruct((128, 128), BF), j...  113 us
    unnamed x14, local copies, waits for them, and re-layouts  9.03 us

profile of v2, /device:TPU:1, one launch (start us, length us, event | category | flops | bytes accessed | tf_op | source)
XLA Modules:
  0.0 122.5 jit_solution(9502960340529751343)
XLA Ops:
  0.6 0.0 copy-start
  0.6 1.2 copy-done
  1.8 0.0 copy-start.1
  1.8 1.2 copy-done.1
  3.0 0.0 copy-start.2
  3.0 0.9 copy-done.2
  3.9 0.0 copy-start.3
  3.9 0.8 copy-done.3
  4.7 0.0 copy-start.4
  4.7 0.7 copy-done.4
  5.4 112.8 %fused.1 = (bf16[128,128]{1,0:T(8,128)(2,1)S(1)}, f32[479,1024]{1,0:T(8,128)S(1)}, f32[1,1024]{1,0:T(1,128)S(1)}, f32[26,256,128]{2,1,0:T(8,128)S(1)}) custom-call(bf16[128,128]{1,0:T(8,128)(2,1)S(1)} %copy-done.3, bf16[26,128,128]{2,1,0:T(8,128)(2,1)S(1)} %bitcast.3, bf16[479,1024]{1,0:T(8,128)(2,1)S(1)} %copy-done, bf16[128,1024]{1,0:T(8,128)(2,1)S(1)} %copy-done.2, ...), custom_call_target="tpu_custom_call" | custom-call | tf_op jit(solution)/shard_map/fused/pallas_call | solution.py:380
  118.2 0.6 copy.13
  118.8 1.3 %copy.14 = f32[479,1024]{1,0:T(8,128)} copy(f32[479,1024]{1,0:T(8,128)S(1)} %get-tuple-element.17) | data formatting | bytes 3923968
  120.1 0.6 copy.15
  120.7 1.7 %copy.16 = f32[26,256,128]{2,1,0:T(8,128)} copy(f32[26,256,128]{2,1,0:T(8,128)S(1)} %get-tuple-element.19) | data formatting | bytes 6815744
Async XLA Ops:
  0.6 1.2 copy-start
  1.8 1.2 copy-start.1
  3.0 0.9 copy-start.2
  3.9 0.8 copy-start.3
  4.7 0.7 copy-start.4

commit v3 on v2

v3 whole, which is shorter than its diff:
```python
import contextlib

import jax
import jax.numpy as jnp
from jax import lax
from jax.experimental import pallas as pl
from jax.experimental.pallas import tpu as pltpu
from jax.sharding import PartitionSpec as P

F32 = jnp.float32
BF = jnp.bfloat16
NT = (((1,), (1,)), ((), ()))
MESH = pl.DeviceIdType.MESH
TABLES = 26
SIZES = (2,) * 13
NC = len(SIZES)
STARTS = tuple(sum(SIZES[:i]) for i in range(NC))
AHEAD = 3
LAG = 2
TOP_AT = -1
HOOKS = {"share": 8, "gather_z": 10, "gather_p": 12, "gather_c": 15}
DIRECT = (NC - 1,)
def scope(name):
    return contextlib.nullcontext()


def coords():
    r = lax.axis_index("rep")
    s = lax.axis_index("shard")
    return (s // 4) % 2 * 2 + r // 2, s % 4, s // 8, r % 2


def plane_peer(q):
    x, y, z, c = coords()
    xl = (x + q // 8) % 2
    xh = (x // 2 + q // 16) % 2
    yy = (y // 2 + q // 4) % 2 * 2 + (y + q // 2) % 2
    return (xl * 2 + (c + q) % 2, z * 8 + xh * 4 + yy)


def z_peer(d):
    return (lax.axis_index("rep"), (lax.axis_index("shard") + 8 * d + 64) % 64)


def rep_peer(i):
    r = lax.axis_index("rep")
    return ((r // 2 + i // 2) % 2 * 2 + (r + i) % 2, lax.axis_index("shard"))


def rcopy(src, dst, ss, rs, to):
    return pltpu.make_async_remote_copy(
        src_ref=src, dst_ref=dst, send_sem=ss, recv_sem=rs, device_id=to, device_id_type=MESH)


def wait_for(reg, sem):
    pltpu.make_async_copy(reg, reg, sem).wait()


def kernel(dense_h, pool_h, w_h, cot_h, idx_h, dgrad, topo, bias, tab,
           dense, pool, w, cot, idx, vt, g, gt, sl, cols, keyt, krow, krv, kt,
           rows, rv, D, zr, fin, tb, tp, r0, s1, r2, pz,
           in_sem, s_send, s_recv, z_send, z_recv, a_send, a_recv, t_send, t_recv):
    x, y, z, c = coords()
    rep = lax.axis_index("rep")
    ins = [pltpu.make_async_copy(a, b, in_sem.at[i]) for i, (a, b) in enumerate(
        ((idx_h, idx), (pool_h, pool), (dense_h, dense), (cot_h, cot), (w_h, w)))]
    for cp in ins:
        cp.start()
    bar = pltpu.get_barrier_semaphore()
    with scope("bar"):
        for q in range(1, 32):
            pl.semaphore_signal(bar, 1, device_id=plane_peer(q), device_id_type=MESH)
        for d in range(1, 8):
            pl.semaphore_signal(bar, 1, device_id=z_peer(d), device_id_type=MESH)
    i0 = lax.broadcasted_iota(jnp.int32, (128, 128), 0)
    i1 = lax.broadcasted_iota(jnp.int32, (128, 128), 1)
    eye = (i0 == i1).astype(F32).astype(BF)
    one = jnp.float32(1)
    zero = jnp.float32(0)

    with scope("in0"):
        ins[0].wait()
    with scope("slots"):
        cols[...] = jnp.zeros_like(cols)
        keys, slots = [], []
        for l in range(2):
            row = idx[:, l, :]
            blk = row >> 6
            xx = ((row >> 10) & 1) * 2 + ((row >> 7) & 1)
            slot = ((xx ^ x) << 7) + ((((row >> 8) & 3) ^ y) << 5) + ((((row >> 6) & 1) ^ c) << 4)
            slot = slot + ((((row >> 11) - z) & 7) << 1)
            keys.append(((row & 63) + 1).astype(F32))
            slots.append(slot.astype(F32))
            cols[32 * l:32 * l + 26] = blk.astype(F32)
            sl[l] = blk.astype(F32)
        ct = cols[...].T
    with scope("rank"):
        sub = lax.broadcasted_iota(jnp.int32, (8, 128), 0)
        lane = lax.broadcasted_iota(jnp.int32, (8, 128), 1)
        for t in range(TABLES):
            b0 = jnp.broadcast_to(sl[0, t:t + 1], (8, 128))
            b1 = jnp.broadcast_to(sl[1, t:t + 1], (8, 128))
            n0 = jnp.zeros((8, 128), F32)
            n1 = n0
            for k in range(16):
                c0 = jnp.broadcast_to(ct[8 * k:8 * k + 8, t:t + 1], (8, 128))
                c1 = jnp.broadcast_to(ct[8 * k:8 * k + 8, 32 + t:33 + t], (8, 128))
                lt = jnp.where(sub + 8 * k < lane, one, zero)
                n0 = n0 + jnp.where(c0 == b0, lt, zero)
                n1 = n1 + jnp.where(c0 == b1, one, zero) + jnp.where(c1 == b1, lt, zero)
            cols[64 + t:65 + t] = jnp.sum(n0, axis=0, keepdims=True)
            cols[96 + t:97 + t] = jnp.sum(n1, axis=0, keepdims=True)
        for l in range(2):
            sl[l] = slots[l] + cols[64 + 32 * l:90 + 32 * l]

    def send_keys():
        for l in range(2):
            cols[32 * l:32 * l + 26] = sl[l]
            cols[64 + 32 * l:90 + 32 * l] = keys[l]
        ct = cols[...].T
        fl = lax.broadcasted_iota(jnp.int32, (8, 128), 1).astype(F32)
        lanes = [fl + jnp.float32(128 * b) for b in range(4)]
        keyt[...] = jnp.zeros_like(keyt)
        for t in range(TABLES):
            acc = [jnp.zeros((8, 128), F32)] * 4
            for k in range(16):
                col = [jnp.broadcast_to(ct[8 * k:8 * k + 8, 32 * j + t:32 * j + t + 1], (8, 128)) for j in range(4)]
                for b in range(4):
                    acc[b] = acc[b] + jnp.where(col[0] == lanes[b], col[2], zero) + jnp.where(col[1] == lanes[b], col[3], zero)
            for b in range(4):
                keyt[t:t + 1, 128 * b:128 * b + 128] = jnp.sum(acc[b], axis=0, keepdims=True)
        krow[...] = keyt[...].T.astype(BF)
        for q in range(1, 32):
            rcopy(krow.at[pl.ds(q * 16, 16)], krv.at[pl.ds(q * 16, 16)], s_send.at[NC], s_recv.at[NC], plane_peer(q)).start()

    with scope("in1"):
        ins[1].wait()
        ins[2].wait()
    with scope("tr"):
        vt[0] = lax.dot_general(eye, dense[...], NT, preferred_element_type=F32)

        def tr(i, _):
            vt[i + 1] = lax.dot_general(eye, pool[i], NT, preferred_element_type=F32)
            return 0

        lax.fori_loop(0, TABLES, tr, 0, unroll=2)
    with scope("in3"):
        ins[3].wait()
        ins[4].wait()
    with scope("gt"):
        gt[0:479] = lax.dot_general(w[...], cot[...], NT, preferred_element_type=F32)
        gt[479:480] = jnp.zeros((1, 128), F32)
    with scope("barwait"):
        pl.semaphore_wait(bar, 38)

    def prow(a, b):
        hi = jnp.maximum(a, b)
        lo = jnp.minimum(a, b)
        return 128 + hi * (hi - 1) // 2 + lo

    def vg(i):
        acc = jnp.zeros((128, 128), F32)
        for j in range(27):
            p = jnp.where(i == j, 479, prow(i, jnp.int32(j)))
            acc = acc + gt[pl.ds(p, 1), :] * vt[j]
        return acc

    s512 = lax.broadcasted_iota(jnp.int32, (512, 128), 0).astype(F32)

    def compute(ch):
        t0, n = STARTS[ch], SIZES[ch]

        def table(t, _):
            v = vg(t + 1).astype(BF)
            p = jnp.where((s512 == sl[0, pl.ds(t, 1), :]) | (s512 == sl[1, pl.ds(t, 1), :]), one, zero)
            rows[t] = lax.dot_general(p.astype(BF), v, NT, preferred_element_type=F32).astype(BF)
            return 0

        lax.fori_loop(t0, t0 + n, table, 0)
        for q in range(1, 32):
            rcopy(rows.at[pl.ds(t0, n), pl.ds(q * 16, 16)], rv.at[pl.ds(t0, n), pl.ds(q * 16, 16)],
                  s_send.at[ch], s_recv.at[ch], plane_peer(q)).start()

    def dense_part():
        d0 = vg(jnp.int32(0)) + gt[0:128]
        dgrad[...] = lax.dot_general(eye, d0.astype(BF), NT, preferred_element_type=F32).astype(BF)

    def core_copy():
        return rcopy(tp.at[1 - c], r0, t_send.at[0], t_recv.at[0], rep_peer(1))

    def top_part():
        g[0:128] = vt[0]
        g[479:480] = jnp.ones((1, 128), F32)

        def gram(i, _):
            va = vt[i]
            for d in range(1, 14):
                j = i + d
                j = jnp.where(j >= 27, j - 27, j)
                g[pl.ds(prow(i, j), 1), :] = jnp.sum(va * vt[j], axis=0, keepdims=True)
            return 0

        lax.fori_loop(0, 27, gram, 0)
        gb = g[...].astype(BF)
        for i in range(2):
            tp[i, 0:480] = jnp.dot(gb, cot[:, 512 * i:512 * i + 512], preferred_element_type=F32).astype(BF)
            tp[i, 480:512] = jnp.zeros((32, 512), BF)
        core_copy().start()

    def top_sum():
        core_copy().wait_recv()
        for k in range(8):
            at = pl.ds(pl.multiple_of((z + k) % 8 * 64, 64), 64)
            v = (tp[c, at].astype(F32) + r0[at].astype(F32)).astype(BF)
            for b in range(4):
                D[TABLES + b, k] = v[:, 128 * b:128 * b + 128]
        zcopy(0, 1, NC).start()
        zcopy(1, 1, NC).start()

    def spot(ref, xx, yy):
        return ref.at[yy, pl.ds(pl.multiple_of(xx * 16, 16), 16)]

    def p_target(q):
        return (x // 2 + q // 8) % 2 * 2 + (x + q // 4) % 2, (y // 2 + q // 2) % 2 * 2 + (y + q) % 2

    def p_share(q):
        return rcopy(spot(s1, *p_target(q)), r2.at[q - 1], t_send.at[2], t_recv.at[2], plane_peer(q * 2))

    def z_gather(d):
        return rcopy(pz, tb.at[c, x * 4 + y, z], t_send.at[3], t_recv.at[3], z_peer(d))

    def p_gather(q):
        reg = tb.at[c, x * 4 + y]
        return rcopy(reg, reg, t_send.at[4], t_recv.at[4], plane_peer(q * 2))

    def core_gather():
        return rcopy(tb.at[c], tb.at[c], t_send.at[5], t_recv.at[5], rep_peer(1))

    def top_share():
        zcopy(0, 4, NC).wait_recv()
        zcopy(1, 4, NC).wait_recv()
        for b in range(4):
            e = TABLES + b
            s1[b] = (D[e, 0].astype(F32) + zr[0, 3, e].astype(F32) + zr[1, 3, e].astype(F32)).astype(BF)
        for q in range(1, 16):
            p_share(q).start()

    def top_gather_z():
        wait_for(r2, t_recv.at[2])
        a = spot(s1, x, y)[...].astype(F32)
        for i in range(15):
            a = a + r2[i].astype(F32)
        pz[...] = a.astype(BF)
        tb[c, x * 4 + y, z] = a.astype(BF)
        for d in range(1, 8):
            z_gather(d).start()

    def top_gather_p():
        wait_for(r2.at[pl.ds(0, 7)], t_recv.at[3])
        for q in range(1, 16):
            p_gather(q).start()

    def top_gather_c():
        wait_for(tb.at[0, pl.ds(0, 15)], t_recv.at[4])
        core_gather().start()

    def span(ch):
        return (STARTS[ch], SIZES[ch]) if ch < NC else (TABLES, 4)

    def zcopy(dirn, step, ch):
        t0, n = span(ch)
        rel = (5 - step) if dirn == 0 else (3 + step)
        lo, sz = (32 * dirn, 32) if step == 1 else (0, 64)
        return rcopy(D.at[pl.ds(t0, n), rel, pl.ds(lo, sz)], zr.at[dirn, step - 1, pl.ds(t0, n), pl.ds(lo, sz)],
                     z_send.at[dirn, step - 1, ch], z_recv.at[dirn, step - 1, ch], z_peer(1 if dirn == 0 else -1))

    def acopy(i, ch):
        t0, n = STARTS[ch], SIZES[ch]
        reg = fin.at[pl.ds(t0, n), pl.ds(pl.multiple_of(rep * 64, 64), 64)]
        return rcopy(reg, reg, a_send.at[i - 1, ch], a_recv.at[i - 1, ch], rep_peer(i))

    def fwd(ch):
        t0, n = STARTS[ch], SIZES[ch]
        reg = fin.at[pl.ds(t0, n), pl.ds(pl.multiple_of((rep + 2) % 4 * 64, 64), 64)]
        return rcopy(reg, reg, a_send.at[2, ch], a_recv.at[2, ch], rep_peer(1))

    def third(ch):
        return acopy(3, ch) if ch in DIRECT else fwd(ch)

    rowi = lax.broadcasted_iota(jnp.int32, (512, 512), 0).astype(F32)

    def gather_keys():
        wait_for(krv.at[pl.ds(16, 496)], s_recv.at[NC])
        krv[0:16] = krow[0:16]
        kk = lax.dot_general(eye, krv[...], NT, preferred_element_type=F32)
        zz = (((lax.broadcasted_iota(jnp.int32, (128, 512), 1) >> 1) & 7) << 6).astype(F32)
        kt[...] = jnp.where(kk > 0.5, kk - 1 + zz, -1.0)

    def gather_rows(ch):
        t0, n = STARTS[ch], SIZES[ch]
        wait_for(rv.at[pl.ds(t0, n), pl.ds(16, 496)], s_recv.at[ch])
        rv[t0:t0 + n, 0:16] = rows[t0:t0 + n, 0:16]

        def acc(t, _):
            oh = jnp.where(rowi == kt[pl.ds(t, 1), :], one, zero).astype(BF)
            D[t] = jnp.dot(oh, rv[t], preferred_element_type=F32).astype(BF).reshape(8, 64, 128)
            return 0

        lax.fori_loop(t0, t0 + n, acc, 0)
        zcopy(0, 1, ch).start()
        zcopy(1, 1, ch).start()

    def zstep(s, ch):
        t0, n = span(ch)
        for dirn in (0, 1):
            zcopy(dirn, s, ch).wait_recv()
            rel = (4 - s) if dirn == 0 else (4 + s)
            lo, sz = (32 * dirn, 32) if s == 1 else (0, 64)
            for e in range(t0, t0 + n):
                D[e, rel, lo:lo + sz] = (D[e, rel, lo:lo + sz].astype(F32) + zr[dirn, s - 1, e, lo:lo + sz].astype(F32)).astype(BF)
            zcopy(dirn, s + 1, ch).start()

    def finish(ch):
        t0, n = STARTS[ch], SIZES[ch]
        zcopy(0, 4, ch).wait_recv()
        zcopy(1, 4, ch).wait_recv()
        for e in range(t0, t0 + n):
            v = D[e, 0].astype(F32) + zr[0, 3, e].astype(F32) + zr[1, 3, e].astype(F32)
            fin[e, pl.ds(pl.multiple_of(rep * 64, 64), 64)] = v.astype(BF)
        acopy(1, ch).start()
        acopy(2, ch).start()
        if ch in DIRECT:
            acopy(3, ch).start()

    def named(name, f, *args):
        with scope(name):
            f(*args)

    chain = list(range(NC))
    chain.insert(TOP_AT + 1, NC)
    named("comp", compute, 0)
    named("comp", compute, 1)
    named("keys", send_keys)
    named("comp", compute, 2)
    named("top", top_part)
    made = AHEAD
    steps = len(chain) + 4 * LAG
    extra = {v: k for k, v in HOOKS.items()}
    acts = {"share": top_share, "gather_z": top_gather_z, "gather_p": top_gather_p, "gather_c": top_gather_c}
    for k in range(max(steps, max(extra) + 1)):
        if made < NC:
            named("comp", compute, made)
            made += 1
        elif made == NC:
            named("dense", dense_part)
            made += 1
        for s in (4, 3, 2, 1):
            i = k - LAG * s
            if 0 <= i < len(chain):
                ch = chain[i]
                if s < 4:
                    named("zs%d_%d" % (s, ch), zstep, s, ch)
                elif ch < NC:
                    named("fin%d" % ch, finish, ch)
        if k < len(chain):
            if chain[k] == NC:
                named("tsum", top_sum)
            else:
                if chain[k] == 0:
                    named("gkeys", gather_keys)
                named("gath%d" % chain[k], gather_rows, chain[k])
        if k in extra:
            named(extra[k], acts[extra[k]])
    with scope("fwd"):
        for ch in range(NC):
            if ch not in DIRECT:
                acopy(2, ch).wait_recv()
                fwd(ch).start()
    with scope("topw"):
        core_gather().wait_recv()
        for cc in range(2):
            for xx in range(4):
                for yy in range(4):
                    for zz in range(8):
                        r, q = zz * 64 + xx * 16, cc * 512 + yy * 128
                        if r < 464:
                            topo[r:r + 16, q:q + 128] = tb[cc, xx * 4 + yy, zz].astype(F32)
                        elif r == 464:
                            v = tb[cc, xx * 4 + yy, zz].astype(F32)
                            topo[r:r + 15, q:q + 128] = v[0:15]
                            bias[q // 128:q // 128 + 1] = v[15:16]
    with scope("tabw"):
        for ch in range(NC):
            t0, n = STARTS[ch], SIZES[ch]
            acopy(1, ch).wait_recv()
            if ch in DIRECT:
                acopy(2, ch).wait_recv()
            third(ch).wait_recv()
            tab[t0:t0 + n] = fin[t0:t0 + n].astype(F32)
    with scope("drain"):
        for ch in range(NC):
            t0, n = STARTS[ch], SIZES[ch]
            acopy(1, ch).wait_send()
            acopy(2, ch).wait_send()
            third(ch).wait_send()
            wait_for(rows.at[pl.ds(t0, n), pl.ds(16, 496)], s_send.at[ch])
        for ch in range(NC + 1):
            for dirn in (0, 1):
                for s in (1, 2, 3, 4):
                    zcopy(dirn, s, ch).wait_send()
        wait_for(krow.at[pl.ds(16, 496)], s_send.at[NC])
        core_copy().wait_send()
        wait_for(r2, t_send.at[2])
        wait_for(r2.at[pl.ds(0, 7)], t_send.at[3])
        wait_for(tb.at[0, pl.ds(0, 15)], t_send.at[4])
        core_gather().wait_send()


def fused_call(dense, pool, w, cot, idx, cid=1, name="fused"):
    vm = pl.BlockSpec(memory_space=pltpu.VMEM)
    hbm = pl.BlockSpec(memory_space=pltpu.HBM)
    dma = pltpu.SemaphoreType.DMA
    V = pltpu.VMEM
    E = TABLES + 4
    return pl.pallas_call(
        kernel,
        out_shape=(
            jax.ShapeDtypeStruct((128, 128), BF),
            jax.ShapeDtypeStruct((479, 1024), F32),
            jax.ShapeDtypeStruct((8, 128), F32),
            jax.ShapeDtypeStruct((TABLES, 256, 128), F32),
        ),
        in_specs=[hbm] * 5,
        out_specs=(vm,) * 4,
        scratch_shapes=[
            V((128, 128), BF), V((TABLES, 128, 128), BF), V((479, 1024), BF), V((128, 1024), BF), V((TABLES, 2, 128), jnp.int32),
            V((27, 128, 128), F32), V((480, 128), F32), V((480, 128), F32), V((2, TABLES, 128), F32), V((128, 128), F32),
            V((128, 512), F32), V((512, 128), BF), V((512, 128), BF), V((128, 512), F32),
            V((TABLES, 512, 128), BF), V((TABLES, 512, 128), BF), V((E, 8, 64, 128), BF), V((2, 4, E, 64, 128), BF),
            V((TABLES, 256, 128), BF),
            V((2, 16, 8, 16, 128), BF), V((2, 512, 512), BF), V((512, 512), BF), V((4, 64, 128), BF), V((15, 16, 128), BF), V((16, 128), BF),
            dma((5,)), dma((NC + 1,)), dma((NC + 1,)), dma((2, 4, NC + 1)), dma((2, 4, NC + 1)), dma((3, NC)), dma((3, NC)), dma((6,)), dma((6,)),
        ],
        compiler_params=pltpu.CompilerParams(collective_id=cid, has_side_effects=True, vmem_limit_bytes=40 * 2**20),
        name=name,
    )(*[pltpu.with_memory_space_constraint(a, pltpu.HBM) for a in (dense, pool, w, cot, idx)])


def result_kernel(dgrad, topo, bias, tab, dgrad_o, topo_o, bias_o, tab_o, sem):
    pairs = [(tab.at[pl.ds(i, 2)], tab_o.at[pl.ds(i, 2)]) for i in range(0, TABLES, 2)]
    pairs += [(topo.at[pl.ds(i, 120)], topo_o.at[pl.ds(i, 120)]) for i in (0, 120, 240)]
    pairs += [(topo.at[pl.ds(360, 119)], topo_o.at[pl.ds(360, 119)]), (dgrad, dgrad_o), (bias, bias_o)]
    copies = [pltpu.make_async_copy(a, b, sem.at[i]) for i, (a, b) in enumerate(pairs)]
    for cp in copies:
        cp.start()
    for cp in copies:
        cp.wait()


def result_call(*arrays):
    vm = pl.BlockSpec(memory_space=pltpu.VMEM)
    hbm = pl.BlockSpec(memory_space=pltpu.HBM)
    return pl.pallas_call(
        result_kernel, out_shape=tuple(jax.ShapeDtypeStruct(a.shape, a.dtype) for a in arrays),
        in_specs=[vm] * 4, out_specs=(hbm,) * 4, scratch_shapes=[pltpu.SemaphoreType.DMA((19,))],
        compiler_params=pltpu.CompilerParams(vmem_limit_bytes=2**20), name="result")(*arrays)


def on_device(dense_out, pooled, top_weight, top_cotangent, indices):
    dgrad, top, bias, table = fused_call(
        dense_out, jnp.transpose(pooled, (1, 0, 2)), top_weight, top_cotangent, jnp.transpose(indices, (1, 2, 0)))
    dgrad, top, bias, table = result_call(dgrad, top, bias, table)
    return dgrad, top, bias.reshape(1024), table


def solution(mesh):
    both = P(("rep", "shard"))
    return jax.shard_map(
        on_device, mesh=mesh, in_specs=(both, both, P(), both, both),
        out_specs=(both, P(), P(), P(None, "shard", None)), check_vma=False)
```

time: 123 us -> 86.2 us (0.70)
  Pallas kernels: 113 us -> 85.2 us
  local copies, waits for them, and re-layouts: 9.03 us -> 0 us
    pallas_call x1, Pallas kernels: 113 us -> 82.7 us  [fused_call(): pl.pallas_call(kernel, out_shape=(jax.ShapeDtypeStruct((128, 128), BF), j...]
    unnamed x14 -> x0, local copies, waits for them, and re-layouts: 9.03 us -> none
    pallas_call x0 -> x1, Pallas kernels: none -> 2.54 us  [result_call(): pl.pallas_call(result_kernel, out_shape=tuple((jax.ShapeDtypeStruct(a.sha...]
where the time goes in v3:
time: 86.2 us; the launch traced here: 86.1 us
  Pallas kernels  85.2 us (99%)
    pallas_call x1, Pallas kernels, fused_call(): pl.pallas_call(kernel, out_shape=(jax.ShapeDtypeStruct((128, 128), BF), j...  82.7 us
    pallas_call x1, Pallas kernels, result_call(): pl.pallas_call(result_kernel, out_shape=tuple((jax.ShapeDtypeStruct(a.sha...  2.54 us

profile of v3, /device:TPU:1, one launch (start us, length us, event | category | flops | bytes accessed | tf_op | source)
XLA Modules:
  0.0 86.1 jit_solution(17693212194203251730)
XLA Ops:
  0.6 82.7 %fused.1 = (bf16[128,128]{1,0:T(8,128)(2,1)S(1)}, f32[479,1024]{1,0:T(8,128)S(1)}, f32[8,128]{1,0:T(8,128)S(1)}, f32[26,256,128]{2,1,0:T(8,128)S(1)}) custom-call(bf16[128,128]{1,0:T(8,128)(2,1)} %dense_h.1, bf16[26,128,128]{2,1,0:T(8,128)(2,1)} %bitcast.3, bf16[479,1024]{1,0:T(8,128)(2,1)} %w_h.1, bf16[128,1024]{1,0:T(8,128)(2,1)} %cot_h.1, ...), custom_call_target="tpu_custom_call" | custom-call | tf_op jit(solution)/shard_map/fused/pallas_call | solution.py:425
  83.3 2.5 %result.1 = (bf16[128,128]{1,0:T(8,128)(2,1)}, f32[479,1024]{1,0:T(8,128)}, f32[8,128]{1,0:T(8,128)}, f32[26,256,128]{2,1,0:T(8,128)}) custom-call(bf16[128,128]{1,0:T(8,128)(2,1)S(1)} %get-tuple-element.12.dgrad, f32[479,1024]{1,0:T(8,128)S(1)} %get-tuple-element.13.topo, f32[8,128]{1,0:T(8,128)S(1)} %get-tuple-element.14.bias, ...), custom_call_target="tpu_custom_call" | custom-call | tf_op jit(solution)/shard_map/result/pallas_call | solution.py:463

commit v4 on v3

--- a/solution.py
+++ b/solution.py
@@ -18,8 +18,10 @@
 AHEAD = 3
 LAG = 2
 TOP_AT = -1
-HOOKS = {"share": 8, "gather_z": 10, "gather_p": 12, "gather_c": 15}
-DIRECT = (NC - 1,)
+HOOKS = {"share": 8, "gather_z": 12, "gather_p": 15, "gather_c": 21}
+RELAYED = NC - 1
+TR = STARTS[RELAYED]
+REST = 2 * TR + 3 * (TABLES - TR)
 def scope(name):
     return contextlib.nullcontext()
 
@@ -59,7 +61,7 @@
 def kernel(dense_h, pool_h, w_h, cot_h, idx_h, dgrad, topo, bias, tab,
            dense, pool, w, cot, idx, vt, g, gt, sl, cols, keyt, krow, krv, kt,
            rows, rv, D, zr, fin, tb, tp, r0, s1, r2, pz,
-           in_sem, s_send, s_recv, z_send, z_recv, a_send, a_recv, t_send, t_recv):
+           in_sem, s_send, k_send, s_recv, z_send, z_recv, a_send, a_recv, t_send, t_recv):
     x, y, z, c = coords()
     rep = lax.axis_index("rep")
     ins = [pltpu.make_async_copy(a, b, in_sem.at[i]) for i, (a, b) in enumerate(
@@ -131,7 +133,7 @@
                 keyt[t:t + 1, 128 * b:128 * b + 128] = jnp.sum(acc[b], axis=0, keepdims=True)
         krow[...] = keyt[...].T.astype(BF)
         for q in range(1, 32):
-            rcopy(krow.at[pl.ds(q * 16, 16)], krv.at[pl.ds(q * 16, 16)], s_send.at[NC], s_recv.at[NC], plane_peer(q)).start()
+            rcopy(krow.at[pl.ds(q * 16, 16)], krv.at[pl.ds(q * 16, 16)], k_send, s_recv.at[NC], plane_peer(q)).start()
 
     with scope("in1"):
         ins[1].wait()
@@ -143,7 +145,7 @@
             vt[i + 1] = lax.dot_general(eye, pool[i], NT, preferred_element_type=F32)
             return 0
 
-        lax.fori_loop(0, TABLES, tr, 0, unroll=2)
+        lax.fori_loop(0, TABLES, tr, 0, unroll=True)
     with scope("in3"):
         ins[3].wait()
         ins[4].wait()
@@ -176,10 +178,10 @@
             rows[t] = lax.dot_general(p.astype(BF), v, NT, preferred_element_type=F32).astype(BF)
             return 0
 
-        lax.fori_loop(t0, t0 + n, table, 0)
+        lax.fori_loop(t0, t0 + n, table, 0, unroll=True)
         for q in range(1, 32):
             rcopy(rows.at[pl.ds(t0, n), pl.ds(q * 16, 16)], rv.at[pl.ds(t0, n), pl.ds(q * 16, 16)],
-                  s_send.at[ch], s_recv.at[ch], plane_peer(q)).start()
+                  s_send, s_recv.at[ch], plane_peer(q)).start()
 
     def dense_part():
         d0 = vg(jnp.int32(0)) + gt[0:128]
@@ -237,26 +239,25 @@
         return rcopy(tb.at[c], tb.at[c], t_send.at[5], t_recv.at[5], rep_peer(1))
 
     def top_share():
-        zcopy(0, 4, NC).wait_recv()
-        zcopy(1, 4, NC).wait_recv()
+        z_wait(4, NC)
         for b in range(4):
             e = TABLES + b
-            s1[b] = (D[e, 0].astype(F32) + zr[0, 3, e].astype(F32) + zr[1, 3, e].astype(F32)).astype(BF)
+            s1[b] = D[e, 0].astype(F32) + zr[0, 3, e].astype(F32) + zr[1, 3, e].astype(F32)
         for q in range(1, 16):
             p_share(q).start()
 
     def top_gather_z():
         wait_for(r2, t_recv.at[2])
-        a = spot(s1, x, y)[...].astype(F32)
+        a = spot(s1, x, y)[...]
         for i in range(15):
-            a = a + r2[i].astype(F32)
+            a = a + r2[i]
         pz[...] = a.astype(BF)
         tb[c, x * 4 + y, z] = a.astype(BF)
         for d in range(1, 8):
             z_gather(d).start()
 
     def top_gather_p():
-        wait_for(r2.at[pl.ds(0, 7)], t_recv.at[3])
+        wait_for(tb.at[0, 0, pl.ds(0, 7)], t_recv.at[3])
         for q in range(1, 16):
             p_gather(q).start()
 
@@ -272,20 +273,22 @@
         rel = (5 - step) if dirn == 0 else (3 + step)
         lo, sz = (32 * dirn, 32) if step == 1 else (0, 64)
         return rcopy(D.at[pl.ds(t0, n), rel, pl.ds(lo, sz)], zr.at[dirn, step - 1, pl.ds(t0, n), pl.ds(lo, sz)],
-                     z_send.at[dirn, step - 1, ch], z_recv.at[dirn, step - 1, ch], z_peer(1 if dirn == 0 else -1))
+                     z_send, z_recv.at[step - 1, ch], z_peer(1 if dirn == 0 else -1))
+
+    def z_wait(step, ch):
+        t0, n = span(ch)
+        reg = zr.at[0, 0, pl.ds(t0, n)] if step == 1 else zr.at[pl.ds(0, 2), step - 1, pl.ds(t0, n)]
+        wait_for(reg, z_recv.at[step - 1, ch])
 
     def acopy(i, ch):
         t0, n = STARTS[ch], SIZES[ch]
         reg = fin.at[pl.ds(t0, n), pl.ds(pl.multiple_of(rep * 64, 64), 64)]
-        return rcopy(reg, reg, a_send.at[i - 1, ch], a_recv.at[i - 1, ch], rep_peer(i))
-
-    def fwd(ch):
-        t0, n = STARTS[ch], SIZES[ch]
-        reg = fin.at[pl.ds(t0, n), pl.ds(pl.multiple_of((rep + 2) % 4 * 64, 64), 64)]
-        return rcopy(reg, reg, a_send.at[2, ch], a_recv.at[2, ch], rep_peer(1))
-
-    def third(ch):
-        return acopy(3, ch) if ch in DIRECT else fwd(ch)
+        got = a_recv.at[0] if i == 2 and ch < RELAYED else a_recv.at[1]
+        return rcopy(reg, reg, a_send, got, rep_peer(i))
+
+    def fwd():
+        reg = fin.at[pl.ds(0, TR), pl.ds(pl.multiple_of((rep + 2) % 4 * 64, 64), 64)]
+        return rcopy(reg, reg, a_send, a_recv.at[1], rep_peer(1))
 
     rowi = lax.broadcasted_iota(jnp.int32, (512, 512), 0).astype(F32)
 
@@ -306,14 +309,14 @@
             D[t] = jnp.dot(oh, rv[t], preferred_element_type=F32).astype(BF).reshape(8, 64, 128)
             return 0
 
-        lax.fori_loop(t0, t0 + n, acc, 0)
+        lax.fori_loop(t0, t0 + n, acc, 0, unroll=True)
         zcopy(0, 1, ch).start()
         zcopy(1, 1, ch).start()
 
     def zstep(s, ch):
         t0, n = span(ch)
+        z_wait(s, ch)
         for dirn in (0, 1):
-            zcopy(dirn, s, ch).wait_recv()
             rel = (4 - s) if dirn == 0 else (4 + s)
             lo, sz = (32 * dirn, 32) if s == 1 else (0, 64)
             for e in range(t0, t0 + n):
@@ -322,14 +325,13 @@
 
     def finish(ch):
         t0, n = STARTS[ch], SIZES[ch]
-        zcopy(0, 4, ch).wait_recv()
-        zcopy(1, 4, ch).wait_recv()
+        z_wait(4, ch)
         for e in range(t0, t0 + n):
             v = D[e, 0].astype(F32) + zr[0, 3, e].astype(F32) + zr[1, 3, e].astype(F32)
             fin[e, pl.ds(pl.multiple_of(rep * 64, 64), 64)] = v.astype(BF)
         acopy(1, ch).start()
         acopy(2, ch).start()
-        if ch in DIRECT:
+        if ch >= RELAYED:
             acopy(3, ch).start()
 
     def named(name, f, *args):
@@ -372,10 +374,8 @@
         if k in extra:
             named(extra[k], acts[extra[k]])
     with scope("fwd"):
-        for ch in range(NC):
-            if ch not in DIRECT:
-                acopy(2, ch).wait_recv()
-                fwd(ch).start()
+        wait_for(fin.at[pl.ds(0, TR), pl.ds(0, 64)], a_recv.at[0])
+        fwd().start()
     with scope("topw"):
         core_gather().wait_recv()
         for cc in range(2):
@@ -390,28 +390,16 @@
                             topo[r:r + 15, q:q + 128] = v[0:15]
                             bias[q // 128:q // 128 + 1] = v[15:16]
     with scope("tabw"):
-        for ch in range(NC):
-            t0, n = STARTS[ch], SIZES[ch]
-            acopy(1, ch).wait_recv()
-            if ch in DIRECT:
-                acopy(2, ch).wait_recv()
-            third(ch).wait_recv()
-            tab[t0:t0 + n] = fin[t0:t0 + n].astype(F32)
+        wait_for(zr.at[0, pl.ds(0, 2), pl.ds(0, REST // 2)], a_recv.at[1])
+        tab[...] = fin[...].astype(F32)
     with scope("drain"):
-        for ch in range(NC):
-            t0, n = STARTS[ch], SIZES[ch]
-            acopy(1, ch).wait_send()
-            acopy(2, ch).wait_send()
-            third(ch).wait_send()
-            wait_for(rows.at[pl.ds(t0, n), pl.ds(16, 496)], s_send.at[ch])
-        for ch in range(NC + 1):
-            for dirn in (0, 1):
-                for s in (1, 2, 3, 4):
-                    zcopy(dirn, s, ch).wait_send()
-        wait_for(krow.at[pl.ds(16, 496)], s_send.at[NC])
+        wait_for(fin.at[pl.ds(0, TABLES), pl.ds(0, 192)], a_send)
+        wait_for(rows.at[pl.ds(0, TABLES), pl.ds(16, 496)], s_send)
+        wait_for(D.at[pl.ds(0, TABLES + 4), pl.ds(0, 7)], z_send)
+        wait_for(krow.at[pl.ds(16, 496)], k_send)
         core_copy().wait_send()
         wait_for(r2, t_send.at[2])
-        wait_for(r2.at[pl.ds(0, 7)], t_send.at[3])
+        wait_for(tb.at[0, 0, pl.ds(0, 7)], t_send.at[3])
         wait_for(tb.at[0, pl.ds(0, 15)], t_send.at[4])
         core_gather().wait_send()
 
@@ -438,8 +426,8 @@
             V((128, 512), F32), V((512, 128), BF), V((512, 128), BF), V((128, 512), F32),
             V((TABLES, 512, 128), BF), V((TABLES, 512, 128), BF), V((E, 8, 64, 128), BF), V((2, 4, E, 64, 128), BF),
             V((TABLES, 256, 128), BF),
-            V((2, 16, 8, 16, 128), BF), V((2, 512, 512), BF), V((512, 512), BF), V((4, 64, 128), BF), V((15, 16, 128), BF), V((16, 128), BF),
-            dma((5,)), dma((NC + 1,)), dma((NC + 1,)), dma((2, 4, NC + 1)), dma((2, 4, NC + 1)), dma((3, NC)), dma((3, NC)), dma((6,)), dma((6,)),
+            V((2, 16, 8, 16, 128), BF), V((2, 512, 512), BF), V((512, 512), BF), V((4, 64, 128), F32), V((15, 16, 128), F32), V((16, 128), BF),
+            dma((5,)), dma(()), dma(()), dma((NC + 1,)), dma(()), dma((4, NC + 1)), dma(()), dma((2,)), dma((6,)), dma((6,)),
         ],
         compiler_params=pltpu.CompilerParams(collective_id=cid, has_side_effects=True, vmem_limit_bytes=40 * 2**20),
         name=name,

time: 86.2 us -> 78.2 us (0.907)
  Pallas kernels: 85.2 us -> 77.3 us
    pallas_call x1, Pallas kernels: 82.7 us -> 74.8 us  [fused_call(): pl.pallas_call(kernel, out_shape=(jax.ShapeDtypeStruct((128, 128), BF), j...]
where the time goes in v4:
time: 78.2 us; the launch traced here: 78.1 us
  Pallas kernels  77.3 us (99%)
  between operations  0.8 us (1%)
    pallas_call x1, Pallas kernels, fused_call(): pl.pallas_call(kernel, out_shape=(jax.ShapeDtypeStruct((128, 128), BF), j...  74.8 us
    pallas_call x1, Pallas kernels, result_call(): pl.pallas_call(result_kernel, out_shape=tuple((jax.ShapeDtypeStruct(a.sha...  2.54 us

profile of v4, /device:TPU:1, one launch (start us, length us, event | category | flops | bytes accessed | tf_op | source)
XLA Modules:
  0.0 78.1 jit_solution(2323175109889257500)
XLA Ops:
  0.6 74.8 %fused.1 = (bf16[128,128]{1,0:T(8,128)(2,1)S(1)}, f32[479,1024]{1,0:T(8,128)S(1)}, f32[8,128]{1,0:T(8,128)S(1)}, f32[26,256,128]{2,1,0:T(8,128)S(1)}) custom-call(bf16[128,128]{1,0:T(8,128)(2,1)} %dense_h.1, bf16[26,128,128]{2,1,0:T(8,128)(2,1)} %bitcast.3, bf16[479,1024]{1,0:T(8,128)(2,1)} %w_h.1, bf16[128,1024]{1,0:T(8,128)(2,1)} %cot_h.1, ...), custom_call_target="tpu_custom_call" | custom-call | tf_op jit(solution)/shard_map/fused/pallas_call | solution.py:413
  75.4 2.5 %result.1 = (bf16[128,128]{1,0:T(8,128)(2,1)}, f32[479,1024]{1,0:T(8,128)}, f32[8,128]{1,0:T(8,128)}, f32[26,256,128]{2,1,0:T(8,128)}) custom-call(bf16[128,128]{1,0:T(8,128)(2,1)S(1)} %get-tuple-element.12.dgrad, f32[479,1024]{1,0:T(8,128)S(1)} %get-tuple-element.13.topo, f32[8,128]{1,0:T(8,128)S(1)} %get-tuple-element.14.bias, ...), custom_call_target="tpu_custom_call" | custom-call | tf_op jit(solution)/shard_map/result/pallas_call | solution.py:451

commit v5 on v4

--- a/solution.py
+++ b/solution.py
@@ -16,11 +16,21 @@
 NC = len(SIZES)
 STARTS = tuple(sum(SIZES[:i]) for i in range(NC))
 AHEAD = 3
-LAG = 2
+GROUPS = (1,) * 13
+CLOSE = {sum(GROUPS[:i + 1]) - 1: sum(GROUPS[:i]) for i in range(len(GROUPS))}
+FLIP = 27
+TOPK = -1
+
+
+def lag_of(i, s):
+    return LAG * s
+
+
+LAG = 4
 TOP_AT = -1
 HOOKS = {"share": 8, "gather_z": 12, "gather_p": 15, "gather_c": 21}
 RELAYED = NC - 1
-TR = STARTS[RELAYED]
+TR = sum(SIZES[:RELAYED])
 REST = 2 * TR + 3 * (TABLES - TR)
 def scope(name):
     return contextlib.nullcontext()
@@ -59,7 +69,7 @@
 
 
 def kernel(dense_h, pool_h, w_h, cot_h, idx_h, dgrad, topo, bias, tab,
-           dense, pool, w, cot, idx, vt, g, gt, sl, cols, keyt, krow, krv, kt,
+           dense, pool, w, cot, idx, vt, g, gt, sl, blks, cols, keyt, krow, krv, kt,
            rows, rv, D, zr, fin, tb, tp, r0, s1, r2, pz,
            in_sem, s_send, k_send, s_recv, z_send, z_recv, a_send, a_recv, t_send, t_recv):
     x, y, z, c = coords()
@@ -94,14 +104,16 @@
             keys.append(((row & 63) + 1).astype(F32))
             slots.append(slot.astype(F32))
             cols[32 * l:32 * l + 26] = blk.astype(F32)
-            sl[l] = blk.astype(F32)
+            blks[l] = blk.astype(F32)
         ct = cols[...].T
-    with scope("rank"):
+    base = slots
+
+    def rank(tables):
         sub = lax.broadcasted_iota(jnp.int32, (8, 128), 0)
         lane = lax.broadcasted_iota(jnp.int32, (8, 128), 1)
-        for t in range(TABLES):
-            b0 = jnp.broadcast_to(sl[0, t:t + 1], (8, 128))
-            b1 = jnp.broadcast_to(sl[1, t:t + 1], (8, 128))
+        for t in tables:
+            b0 = jnp.broadcast_to(blks[0, t:t + 1], (8, 128))
+            b1 = jnp.broadcast_to(blks[1, t:t + 1], (8, 128))
             n0 = jnp.zeros((8, 128), F32)
             n1 = n0
             for k in range(16):
@@ -110,10 +122,11 @@
                 lt = jnp.where(sub + 8 * k < lane, one, zero)
                 n0 = n0 + jnp.where(c0 == b0, lt, zero)
                 n1 = n1 + jnp.where(c0 == b1, one, zero) + jnp.where(c1 == b1, lt, zero)
-            cols[64 + t:65 + t] = jnp.sum(n0, axis=0, keepdims=True)
-            cols[96 + t:97 + t] = jnp.sum(n1, axis=0, keepdims=True)
-        for l in range(2):
-            sl[l] = slots[l] + cols[64 + 32 * l:90 + 32 * l]
+            sl[0, t:t + 1] = base[0][t:t + 1] + jnp.sum(n0, axis=0, keepdims=True)
+            sl[1, t:t + 1] = base[1][t:t + 1] + jnp.sum(n1, axis=0, keepdims=True)
+
+    with scope("rank"):
+        rank(range(SIZES[0]))
 
     def send_keys():
         for l in range(2):
@@ -179,9 +192,12 @@
             return 0
 
         lax.fori_loop(t0, t0 + n, table, 0, unroll=True)
-        for q in range(1, 32):
-            rcopy(rows.at[pl.ds(t0, n), pl.ds(q * 16, 16)], rv.at[pl.ds(t0, n), pl.ds(q * 16, 16)],
-                  s_send, s_recv.at[ch], plane_peer(q)).start()
+        if ch in CLOSE:
+            g0 = STARTS[CLOSE[ch]]
+            n = t0 + n - g0
+            for q in range(1, 32):
+                rcopy(rows.at[pl.ds(g0, n), pl.ds(q * 16, 16)], rv.at[pl.ds(g0, n), pl.ds(q * 16, 16)],
+                      s_send, s_recv.at[ch], plane_peer(q)).start()
 
     def dense_part():
         d0 = vg(jnp.int32(0)) + gt[0:128]
@@ -202,7 +218,7 @@
                 g[pl.ds(prow(i, j), 1), :] = jnp.sum(va * vt[j], axis=0, keepdims=True)
             return 0
 
-        lax.fori_loop(0, 27, gram, 0)
+        lax.fori_loop(0, 27, gram, 0, unroll=3)
         gb = g[...].astype(BF)
         for i in range(2):
             tp[i, 0:480] = jnp.dot(gb, cot[:, 512 * i:512 * i + 512], preferred_element_type=F32).astype(BF)
@@ -301,7 +317,10 @@
 
     def gather_rows(ch):
         t0, n = STARTS[ch], SIZES[ch]
-        wait_for(rv.at[pl.ds(t0, n), pl.ds(16, 496)], s_recv.at[ch])
+        for last, first in CLOSE.items():
+            if first == ch:
+                end = STARTS[last] + SIZES[last]
+                wait_for(rv.at[pl.ds(t0, end - t0), pl.ds(16, 496)], s_recv.at[last])
         rv[t0:t0 + n, 0:16] = rows[t0:t0 + n, 0:16]
 
         def acc(t, _):
@@ -341,37 +360,44 @@
     chain = list(range(NC))
     chain.insert(TOP_AT + 1, NC)
     named("comp", compute, 0)
+    named("rank", rank, range(SIZES[0], TABLES))
     named("comp", compute, 1)
     named("keys", send_keys)
     named("comp", compute, 2)
-    named("top", top_part)
+    if TOPK < 0:
+        named("top", top_part)
     made = AHEAD
-    steps = len(chain) + 4 * LAG
     extra = {v: k for k, v in HOOKS.items()}
     acts = {"share": top_share, "gather_z": top_gather_z, "gather_p": top_gather_p, "gather_c": top_gather_c}
-    for k in range(max(steps, max(extra) + 1)):
-        if made < NC:
-            named("comp", compute, made)
-            made += 1
-        elif made == NC:
-            named("dense", dense_part)
-            made += 1
-        for s in (4, 3, 2, 1):
-            i = k - LAG * s
-            if 0 <= i < len(chain):
-                ch = chain[i]
-                if s < 4:
-                    named("zs%d_%d" % (s, ch), zstep, s, ch)
-                elif ch < NC:
-                    named("fin%d" % ch, finish, ch)
-        if k < len(chain):
+    halves = {}
+    for i, ch in enumerate(chain):
+        for s in (1, 2, 3, 4):
+            halves.setdefault(2 * i + lag_of(i, s), []).append((i, s, ch))
+    n = max(max(halves), 2 * max(extra) + 1) + 1
+    for h in range(n):
+        k = h // 2
+        if h % 2 == 0:
+            if made < NC:
+                named("comp", compute, made)
+                made += 1
+            elif made == NC:
+                named("dense", dense_part)
+                made += 1
+        for i, s, ch in sorted(halves.get(h, []), reverse=h >= FLIP):
+            if s < 4:
+                named("zs%d_%d" % (s, ch), zstep, s, ch)
+            elif ch < NC:
+                named("fin%d" % ch, finish, ch)
+        if h % 2 == 0 and k < len(chain):
             if chain[k] == NC:
                 named("tsum", top_sum)
             else:
                 if chain[k] == 0:
                     named("gkeys", gather_keys)
                 named("gath%d" % chain[k], gather_rows, chain[k])
-        if k in extra:
+        if h == 2 * TOPK:
+            named("top", top_part)
+        if h % 2 == 1 and k in extra:
             named(extra[k], acts[extra[k]])
     with scope("fwd"):
         wait_for(fin.at[pl.ds(0, TR), pl.ds(0, 64)], a_recv.at[0])
@@ -422,7 +448,7 @@
         out_specs=(vm,) * 4,
         scratch_shapes=[
             V((128, 128), BF), V((TABLES, 128, 128), BF), V((479, 1024), BF), V((128, 1024), BF), V((TABLES, 2, 128), jnp.int32),
-            V((27, 128, 128), F32), V((480, 128), F32), V((480, 128), F32), V((2, TABLES, 128), F32), V((128, 128), F32),
+            V((27, 128, 128), F32), V((480, 128), F32), V((480, 128), F32), V((2, TABLES, 128), F32), V((2, TABLES, 128), F32), V((128, 128), F32),
             V((128, 512), F32), V((512, 128), BF), V((512, 128), BF), V((128, 512), F32),
             V((TABLES, 512, 128), BF), V((TABLES, 512, 128), BF), V((E, 8, 64, 128), BF), V((2, 4, E, 64, 128), BF),
             V((TABLES, 256, 128), BF),

time: 78.2 us -> 77.2 us (0.987)
  Pallas kernels: 77.3 us -> 76.3 us
    pallas_call x1, Pallas kernels: 74.8 us -> 73.7 us  [fused_call(): pl.pallas_call(kernel, out_shape=(jax.ShapeDtypeStruct((128, 128), BF), j...]
where the time goes in v5:
time: 77.2 us; the launch traced here: 77.1 us
  Pallas kernels  76.3 us (99%)
  between operations  0.8 us (1%)
    pallas_call x1, Pallas kernels, fused_call(): pl.pallas_call(kernel, out_shape=(jax.ShapeDtypeStruct((128, 128), BF), j...  73.7 us
    pallas_call x1, Pallas kernels, result_call(): pl.pallas_call(result_kernel, out_shape=tuple((jax.ShapeDtypeStruct(a.sha...  2.54 us

profile of v5, /device:TPU:1, one launch (start us, length us, event | category | flops | bytes accessed | tf_op | source)
XLA Modules:
  0.0 77.1 jit_solution(11577043633428181400)
XLA Ops:
  0.6 73.7 %fused.1 = (bf16[128,128]{1,0:T(8,128)(2,1)S(1)}, f32[479,1024]{1,0:T(8,128)S(1)}, f32[8,128]{1,0:T(8,128)S(1)}, f32[26,256,128]{2,1,0:T(8,128)S(1)}) custom-call(bf16[128,128]{1,0:T(8,128)(2,1)} %dense_h.1, bf16[26,128,128]{2,1,0:T(8,128)(2,1)} %bitcast.3, bf16[479,1024]{1,0:T(8,128)(2,1)} %w_h.1, bf16[128,1024]{1,0:T(8,128)(2,1)} %cot_h.1, ...), custom_call_target="tpu_custom_call" | custom-call | tf_op jit(solution)/shard_map/fused/pallas_call | solution.py:439
  74.4 2.5 %result.1 = (bf16[128,128]{1,0:T(8,128)(2,1)}, f32[479,1024]{1,0:T(8,128)}, f32[8,128]{1,0:T(8,128)}, f32[26,256,128]{2,1,0:T(8,128)}) custom-call(bf16[128,128]{1,0:T(8,128)(2,1)S(1)} %get-tuple-element.12.dgrad, f32[479,1024]{1,0:T(8,128)S(1)} %get-tuple-element.13.topo, f32[8,128]{1,0:T(8,128)S(1)} %get-tuple-element.14.bias, ...), custom_call_target="tpu_custom_call" | custom-call | tf_op jit(solution)/shard_map/result/pallas_call | solution.py:477

commit v6 on v5

--- a/solution.py
+++ b/solution.py
@@ -28,7 +28,7 @@
 
 LAG = 4
 TOP_AT = -1
-HOOKS = {"share": 8, "gather_z": 12, "gather_p": 15, "gather_c": 21}
+HOOKS = {"share": 8, "gather_z": 12, "gather_p": 14, "gather_c": 21}
 RELAYED = NC - 1
 TR = sum(SIZES[:RELAYED])
 REST = 2 * TR + 3 * (TABLES - TR)

time: 77.2 us -> 76.6 us (level)
  no operation moved by 1% of the time
where the time goes in v6:
time: 76.6 us; the launch traced here: 76.5 us
  Pallas kernels  75.7 us (99%)
  between operations  0.8 us (1%)
    pallas_call x1, Pallas kernels, fused_call(): pl.pallas_call(kernel, out_shape=(jax.ShapeDtypeStruct((128, 128), BF), j...  73.2 us
    pallas_call x1, Pallas kernels, result_call(): pl.pallas_call(result_kernel, out_shape=tuple((jax.ShapeDtypeStruct(a.sha...  2.54 us

profile of v6, /device:TPU:1, one launch (start us, length us, event | category | flops | bytes accessed | tf_op | source)
XLA Modules:
  0.0 76.5 jit_solution(2573831464559607480)
XLA Ops:
  0.6 73.2 %fused.1 = (bf16[128,128]{1,0:T(8,128)(2,1)S(1)}, f32[479,1024]{1,0:T(8,128)S(1)}, f32[8,128]{1,0:T(8,128)S(1)}, f32[26,256,128]{2,1,0:T(8,128)S(1)}) custom-call(bf16[128,128]{1,0:T(8,128)(2,1)} %dense_h.1, bf16[26,128,128]{2,1,0:T(8,128)(2,1)} %bitcast.3, bf16[479,1024]{1,0:T(8,128)(2,1)} %w_h.1, bf16[128,1024]{1,0:T(8,128)(2,1)} %cot_h.1, ...), custom_call_target="tpu_custom_call" | custom-call | tf_op jit(solution)/shard_map/fused/pallas_call | solution.py:439
  73.8 2.5 %result.1 = (bf16[128,128]{1,0:T(8,128)(2,1)}, f32[479,1024]{1,0:T(8,128)}, f32[8,128]{1,0:T(8,128)}, f32[26,256,128]{2,1,0:T(8,128)}) custom-call(bf16[128,128]{1,0:T(8,128)(2,1)S(1)} %get-tuple-element.12.dgrad, f32[479,1024]{1,0:T(8,128)S(1)} %get-tuple-element.13.topo, f32[8,128]{1,0:T(8,128)S(1)} %get-tuple-element.14.bias, ...), custom_call_target="tpu_custom_call" | custom-call | tf_op jit(solution)/shard_map/result/pallas_call | solution.py:477

commit v7 on v6

--- a/solution.py
+++ b/solution.py
@@ -18,7 +18,7 @@
 AHEAD = 3
 GROUPS = (1,) * 13
 CLOSE = {sum(GROUPS[:i + 1]) - 1: sum(GROUPS[:i]) for i in range(len(GROUPS))}
-FLIP = 27
+FLIP = 30
 TOPK = -1
 
 
@@ -28,7 +28,7 @@
 
 LAG = 4
 TOP_AT = -1
-HOOKS = {"share": 8, "gather_z": 12, "gather_p": 14, "gather_c": 21}
+HOOKS = {"share": 8, "gather_z": 12, "gather_p": 14, "gather_c": 20}
 RELAYED = NC - 1
 TR = sum(SIZES[:RELAYED])
 REST = 2 * TR + 3 * (TABLES - TR)
@@ -461,14 +461,14 @@
 
 
 def result_kernel(dgrad, topo, bias, tab, dgrad_o, topo_o, bias_o, tab_o, sem):
-    pairs = [(tab.at[pl.ds(i, 2)], tab_o.at[pl.ds(i, 2)]) for i in range(0, TABLES, 2)]
-    pairs += [(topo.at[pl.ds(i, 120)], topo_o.at[pl.ds(i, 120)]) for i in (0, 120, 240)]
-    pairs += [(topo.at[pl.ds(360, 119)], topo_o.at[pl.ds(360, 119)]), (dgrad, dgrad_o), (bias, bias_o)]
-    copies = [pltpu.make_async_copy(a, b, sem.at[i]) for i, (a, b) in enumerate(pairs)]
-    for cp in copies:
-        cp.start()
-    for cp in copies:
-        cp.wait()
+    for i in range(0, TABLES, 2):
+        pltpu.make_async_copy(tab.at[pl.ds(i, 2)], tab_o.at[pl.ds(i, 2)], sem.at[0]).start()
+    for i, n in ((0, 120), (120, 120), (240, 120), (360, 119)):
+        pltpu.make_async_copy(topo.at[pl.ds(i, n)], topo_o.at[pl.ds(i, n)], sem.at[1]).start()
+    pltpu.make_async_copy(dgrad, dgrad_o, sem.at[2]).start()
+    pltpu.make_async_copy(bias, bias_o, sem.at[3]).start()
+    for i, (a, b) in enumerate(((tab, tab_o), (topo, topo_o), (dgrad, dgrad_o), (bias, bias_o))):
+        pltpu.make_async_copy(a, b, sem.at[i]).wait()
 
 
 def result_call(*arrays):
@@ -476,7 +476,7 @@
     hbm = pl.BlockSpec(memory_space=pltpu.HBM)
     return pl.pallas_call(
         result_kernel, out_shape=tuple(jax.ShapeDtypeStruct(a.shape, a.dtype) for a in arrays),
-        in_specs=[vm] * 4, out_specs=(hbm,) * 4, scratch_shapes=[pltpu.SemaphoreType.DMA((19,))],
+        in_specs=[vm] * 4, out_specs=(hbm,) * 4, scratch_shapes=[pltpu.SemaphoreType.DMA((4,))],
         compiler_params=pltpu.CompilerParams(vmem_limit_bytes=2**20), name="result")(*arrays)
 
 

time: 76.6 us -> 76.5 us (level)
  no operation moved by 1% of the time
where the time goes in v7:
time: 76.5 us; the launch traced here: 76.4 us
  Pallas kernels  75.6 us (99%)
  between operations  0.8 us (1%)
    pallas_call x1, Pallas kernels, fused_call(): pl.pallas_call(kernel, out_shape=(jax.ShapeDtypeStruct((128, 128), BF), j...  73.2 us
    pallas_call x1, Pallas kernels, result_call(): pl.pallas_call(result_kernel, out_shape=tuple((jax.ShapeDtypeStruct(a.sha...  2.41 us

profile of v7, /device:TPU:1, one launch (start us, length us, event | category | flops | bytes accessed | tf_op | source)
XLA Modules:
  0.0 76.4 jit_solution(16331977484997814950)
XLA Ops:
  0.6 73.2 %fused.1 = (bf16[128,128]{1,0:T(8,128)(2,1)S(1)}, f32[479,1024]{1,0:T(8,128)S(1)}, f32[8,128]{1,0:T(8,128)S(1)}, f32[26,256,128]{2,1,0:T(8,128)S(1)}) custom-call(bf16[128,128]{1,0:T(8,128)(2,1)} %dense_h.1, bf16[26,128,128]{2,1,0:T(8,128)(2,1)} %bitcast.3, bf16[479,1024]{1,0:T(8,128)(2,1)} %w_h.1, bf16[128,1024]{1,0:T(8,128)(2,1)} %cot_h.1, ...), custom_call_target="tpu_custom_call" | custom-call | tf_op jit(solution)/shard_map/fused/pallas_call | solution.py:439
  73.8 2.4 %result.1 = (bf16[128,128]{1,0:T(8,128)(2,1)}, f32[479,1024]{1,0:T(8,128)}, f32[8,128]{1,0:T(8,128)}, f32[26,256,128]{2,1,0:T(8,128)}) custom-call(bf16[128,128]{1,0:T(8,128)(2,1)S(1)} %get-tuple-element.12.dgrad, f32[479,1024]{1,0:T(8,128)S(1)} %get-tuple-element.13.topo, f32[8,128]{1,0:T(8,128)S(1)} %get-tuple-element.14.bias, ...), custom_call_target="tpu_custom_call" | custom-call | tf_op jit(solution)/shard_map/result/pallas_call | solution.py:477

commit v8 on v6

--- a/solution.py
+++ b/solution.py
@@ -218,7 +218,7 @@
                 g[pl.ds(prow(i, j), 1), :] = jnp.sum(va * vt[j], axis=0, keepdims=True)
             return 0
 
-        lax.fori_loop(0, 27, gram, 0, unroll=3)
+        lax.fori_loop(0, 27, gram, 0, unroll=9)
         gb = g[...].astype(BF)
         for i in range(2):
             tp[i, 0:480] = jnp.dot(gb, cot[:, 512 * i:512 * i + 512], preferred_element_type=F32).astype(BF)

time: 76.6 us -> 76.7 us (level)
  no operation moved by 1% of the time
where the time goes in v8:
time: 76.7 us; the launch traced here: 76.6 us
  Pallas kernels  75.8 us (99%)
  between operations  0.8 us (1%)
    pallas_call x1, Pallas kernels, fused_call(): pl.pallas_call(kernel, out_shape=(jax.ShapeDtypeStruct((128, 128), BF), j...  73.2 us
    pallas_call x1, Pallas kernels, result_call(): pl.pallas_call(result_kernel, out_shape=tuple((jax.ShapeDtypeStruct(a.sha...  2.54 us

profile of v8, /device:TPU:1, one launch (start us, length us, event | category | flops | bytes accessed | tf_op | source)
XLA Modules:
  0.0 76.6 jit_solution(17594868883161761661)
XLA Ops:
  0.6 73.2 %fused.1 = (bf16[128,128]{1,0:T(8,128)(2,1)S(1)}, f32[479,1024]{1,0:T(8,128)S(1)}, f32[8,128]{1,0:T(8,128)S(1)}, f32[26,256,128]{2,1,0:T(8,128)S(1)}) custom-call(bf16[128,128]{1,0:T(8,128)(2,1)} %dense_h.1, bf16[26,128,128]{2,1,0:T(8,128)(2,1)} %bitcast.3, bf16[479,1024]{1,0:T(8,128)(2,1)} %w_h.1, bf16[128,1024]{1,0:T(8,128)(2,1)} %cot_h.1, ...), custom_call_target="tpu_custom_call" | custom-call | tf_op jit(solution)/shard_map/fused/pallas_call | solution.py:439
  73.9 2.5 %result.1 = (bf16[128,128]{1,0:T(8,128)(2,1)}, f32[479,1024]{1,0:T(8,128)}, f32[8,128]{1,0:T(8,128)}, f32[26,256,128]{2,1,0:T(8,128)}) custom-call(bf16[128,128]{1,0:T(8,128)(2,1)S(1)} %get-tuple-element.12.dgrad, f32[479,1024]{1,0:T(8,128)S(1)} %get-tuple-element.13.topo, f32[8,128]{1,0:T(8,128)S(1)} %get-tuple-element.14.bias, ...), custom_call_target="tpu_custom_call" | custom-call | tf_op jit(solution)/shard_map/result/pallas_call | solution.py:477
